TPU v7x, 32 devices: a whole 2x2x4 slice. The times are simulated.
32 devices in a mesh: dp: 4 (over z), row: 4 (over y, x), col: 2 (over core).
Axes of the slice: x: 2, y: 2, z: 4, core: 2. Of those that a mesh axis runs over, the one named last changes fastest.
Arguments:
- tokens: bfloat16 [2048, 1024], P('dp', ('row', 'col')), may hold values from -7.5 to 7.5
- out_grad: bfloat16 [2048, 1024], P('dp', ('row', 'col')), may hold values from -6 to 6
- doc_ids: int32 [2048], P('dp'), may hold values from 0 to 3, never falling along the last dimension, each value on 1 to 1024 neighbouring positions
- expert_ids: int32 [2048, 8], P('dp'), may hold values from 0 to 31, all different within a row
- gain_attn: bfloat16 [1024], P(('row', 'col')), may hold values from 0.5 to 1.5
- w_query: bfloat16 [1024, 1024], P(None, ('row', 'col')), may hold values from -1.1015625 to 1.1015625
- w_key_value: bfloat16 [1024, 8, 128], P(None, ('row', 'col')), may hold values from -0.1875 to 0.1875
- w_output: bfloat16 [1024, 1024], P(('row', 'col')), may hold values from -6 to 6
- gain_moe: bfloat16 [1024], P(('row', 'col')), may hold values from 0.5 to 1.5
- w_router: bfloat16 [1024, 32], P(('row', 'col')), may hold values from -2.75 to 2.75
- w_expert_in: bfloat16 [32, 1024, 2, 512], P('row', None, None, 'col'), may hold values from -0.1875 to 0.1875
- w_expert_out: bfloat16 [32, 512, 1024], P('row', 'col'), may hold values from -4 to 4
Outputs:
- block_out: bfloat16 [2048, 1024], P('dp', ('row', 'col'))
- in_grad: bfloat16 [2048, 1024], P('dp', ('row', 'col'))
- grad_gain_attn: float32 [1024], P(('row', 'col'))
- grad_query: float32 [1024, 1024], P(None, ('row', 'col'))
- grad_key_value: float32 [1024, 8, 128], P(None, ('row', 'col'))
- grad_output: float32 [1024, 1024], P(('row', 'col'))
- grad_gain_moe: float32 [1024], P(('row', 'col'))
- grad_router: float32 [1024, 32], P(('row', 'col'))
- grad_expert_in: float32 [32, 1024, 2, 512], P('row', None, None, 'col')
- grad_expert_out: float32 [32, 512, 1024], P('row', 'col')
Inputs may be any that keep to these rules, and one draw needn't show every extreme that they name: `doc_ids`: never falling along the token stream; every document has 1 to 1024 tokens and one has exactly 1024. `expert_ids`: each row names 8 different experts; every expert is named by some row.
All inputs are finite; a program needn't handle non-finite values.
Results may differ from a plain program's by a relative error of at most 0.02555.
Values may be sent and summed in bfloat16 or wider, within the bound.
A program may use at most 192 MiB of HBM per device.

v0:
```python
import functools
import itertools
import math

import jax
import jax.numpy as jnp
from jax import lax
from jax.experimental import pallas as pl
from jax.experimental.pallas import tpu as pltpu
from jax.sharding import PartitionSpec as P

LONGEST = 4096
HIGH = lax.Precision.HIGHEST
EPSILON = 1e-05
RESIDUAL_SCALE = 0.22
SCORE_SCALE = 0.015625
ROPE_BASE = 10000.0
MASKED = -1e30
MESH = pl.DeviceIdType.MESH
GROUP = ("row", "col")
EVERY = ("dp", "row", "col")
LANES = 128
HBM = pl.BlockSpec(memory_space=pl.ANY)
FULL = pl.BlockSpec(memory_space=pltpu.VMEM)
TURN = LANES // 4


class Moves:
    def __init__(self, sizes, kinds, sources, targets, sems):
        self.sizes, self.kinds = sizes, kinds
        self.sources, self.targets = sources, targets
        self.send_sem, self.recv_sem, self.local_sem = sems

    def place(self):
        row, col, layer = lax.axis_index("row"), lax.axis_index("col"), lax.axis_index("dp")
        return row, col, layer, row * self.sizes[1] + col

    def member(self, index):
        rows, cols, depth = self.sizes
        return {"row": index // cols, "col": lax.rem(index, cols)}

    def across(self, row):
        low = lax.rem(row, 2)
        return row + 1 - 2 * low, lax.rem(row + 2, 4), lax.rem(row + 3 - 2 * low, 4)

    def barrier(self):
        rows, cols, depth = self.sizes
        row, col, layer, me = self.place()
        group = rows * cols
        names = [kind[0] for kind in self.kinds]
        barrier = pltpu.get_barrier_semaphore()
        partners = []
        if "swap" in names or "share" in names:
            for k in range(1, group):
                partners.append(self.member(lax.rem(me + k, group)))
        elif "gather" in names:
            for other in self.across(row)[:2]:
                partners.append({"row": other})
            for k in range(1, cols):
                partners.append({"col": lax.rem(col + k, cols)})
        shifts = set()
        for kind in self.kinds:
            if kind[0] == "shift":
                for d in kind[1]:
                    shifts |= {d % depth, -d % depth}
            elif kind[0] in ("turn", "collect"):
                shifts |= set(range(1, depth))
        for k in sorted(shifts - {0}):
            partners.append({"dp": lax.rem(layer + k, depth)})
        ends = [(layer > 0, layer - 1), (layer < depth - 1, layer + 1)]
        ends = ends if "line" in names and not shifts else []
        for partner in partners:
            pl.semaphore_signal(barrier, inc=1, device_id=partner, device_id_type=MESH)
        for there, other in ends:

            @pl.when(there)
            def _(device={"dp": other}):
                pl.semaphore_signal(barrier, inc=1, device_id=device, device_id_type=MESH)

        expected = len(partners)
        for there, _ in ends:
            expected = expected + there.astype(jnp.int32)
        pl.semaphore_wait(barrier, expected)

    def plan(self, only):
        rows, cols, depth = self.sizes
        row, col, layer, me = self.place()
        group = rows * cols
        slots = iter(range(self.send_sem.shape[0]))
        starts, relays, sends, arrivals, local = [], [], [], [], []

        def remote(source, target, device, slot=None):
            slot = next(slots) if slot is None else slot
            return functools.partial(
                pltpu.make_async_remote_copy,
                src_ref=source,
                dst_ref=target,
                send_sem=self.send_sem.at[slot],
                recv_sem=self.recv_sem.at[slot],
                device_id=device,
                device_id_type=MESH,
            )

        for index, (kind, source, target) in enumerate(
            zip(self.kinds, self.sources, self.targets)
        ):
            item = [], [], [], [], []
            begin, follow, sent, got, stay = item

            def keep(source, target):
                sem = self.local_sem.at[index]
                stay.append(functools.partial(pltpu.make_async_copy, source, target, sem))

            def direct(source, target, device):
                copy = None, remote(source, target, device)
                begin.append(copy)
                sent.append(copy)
                got.append(copy)

            if kind[0] == "gather":
                second, parts = kind[1:]
                size = source.shape[0] // parts
                beside, above, away = self.across(row)

                def at(other, part, piece=None):
                    member = other * cols + col
                    first, length, deep = part * size, size, ()
                    if piece is not None and size % 2 == 0:
                        length = size // 2
                        first = first + piece * length
                    elif piece is not None:
                        inner = source.shape[1] // 2
                        deep = (pl.ds(piece * inner, inner),)
                    some = pl.ds(first, length)
                    return target.at[(some, member) + deep if second else (member, some) + deep]

                def to_mates(piece):
                    made = []
                    for j in range(1, cols):
                        copy = None, remote(piece, piece, {"col": lax.rem(col + j, cols)})
                        made.append(copy)
                        sent.append(copy)
                        got.append(copy)
                    return made

                for part in range(parts):
                    some = source.at[pl.ds(part * size, size)]
                    ways = []
                    for near, other, piece in ((beside, above, 0), (above, beside, 1)):
                        first = None, remote(some, at(row, part), {"row": near})
                        passed = at(near, part, piece)
                        onward = None, remote(passed, passed, {"row": other})
                        begin.append(first)
                        sent.extend([first, onward])
                        ways.append((near, piece, first, onward))
                    for near, piece, first, onward in ways:
                        nexts = [onward] + to_mates(at(near, part))
                        follow.append((2 + 3 * part, 0, None, first[1], nexts))
                    for near, piece, first, onward in ways:
                        nexts = to_mates(at(away, part, piece))
                        follow.append((2 + 3 * parts + part, 1, None, onward[1], nexts))
                    for j in range(1, cols):
                        direct(some, at(row, part), {"col": lax.rem(col + j, cols)})
                keep(source, target.at[:, me] if second else target.at[me])
            elif kind[0] in ("swap", "share"):
                for k in range(1, group):
                    other = lax.rem(me + k, group)
                    piece = source.at[other] if kind[0] == "swap" else source
                    direct(piece, target.at[me], self.member(other))
                keep(source.at[me] if kind[0] == "swap" else source, target.at[me])
            elif kind[0] in ("turn", "collect"):
                for k in range(1, depth):
                    other = lax.rem(layer + k, depth)
                    piece = source.at[other] if kind[0] == "turn" else source
                    direct(piece, target.at[layer], {"dp": other})
                keep(source.at[layer] if kind[0] == "turn" else source, target.at[layer])
            elif kind[0] == "line":
                absolute, parts = kind[1:]
                size = source.shape[0] // parts
                for part, way in itertools.product(range(parts), (1, -1)):
                    behind = layer if way == 1 else depth - 1 - layer
                    onward = layer + way
                    more = (onward >= 0) & (onward < depth)
                    mine = [next(slots) for _ in range(1, depth)]
                    some = pl.ds(part * size, size)

                    def held(step, where, way=way, some=some):
                        if step == 0:
                            return source.at[some]
                        if absolute:
                            return target.at[where - way * step, some]
                        return target.at[step - 1 if way == 1 else depth - 1 - step, some]

                    def sending(step, onward=onward, mine=mine, held=held):
                        device = {"dp": onward}
                        return remote(
                            held(step - 1, layer), held(step, onward), device, mine[step - 1]
                        )

                    begin.append((more, sending(1)))
                    for step in range(1, depth):
                        sent.append((more & (behind >= step - 1), sending(step)))
                        block = held(step, layer)
                        arrival = remote(block, block, {"dp": onward}, mine[step - 1])
                        nexts = [(more, sending(step + 1))] if step + 1 < depth else []
                        when = 4 * step + part
                        follow.append((when, step - 1, behind >= step, arrival, nexts))
                if absolute:
                    keep(source, target.at[layer])
            else:
                for at_slot, d in enumerate(kind[1]):
                    piece = source.at[at_slot] if kind[2] else source
                    direct(piece, target.at[at_slot], {"dp": lax.rem(layer + d % depth, depth)})
            if only is None or index in only:
                starts += begin
                relays += follow
                sends += sent
                arrivals += got
                local += stay
        return starts, sorted(relays, key=lambda entry: entry[0]), sends, arrivals, local

    def given(self, condition, action):
        if condition is None:
            action()
        else:
            pl.when(condition)(action)

    def start(self, only=None):
        starts, _, _, _, local = self.plan(only)
        for condition, copy in starts:
            self.given(condition, lambda copy=copy: copy().start())
        for copy in local:
            copy().start()

    def relay(self, only=None, stages=None):
        for _, stage, condition, copy, nexts in self.plan(only)[1]:
            if stages is not None and stage not in stages:
                continue

            def action(copy=copy, nexts=nexts):
                copy().wait_recv()
                for more, follower in nexts:
                    self.given(more, lambda follower=follower: follower().start())

            self.given(condition, action)

    def finish(self, only=None):
        _, _, sends, arrivals, local = self.plan(only)
        for condition, copy in arrivals:
            self.given(condition, lambda copy=copy: copy().wait_recv())
        for condition, copy in sends:
            self.given(condition, lambda copy=copy: copy().wait_send())
        for copy in local:
            copy().wait()


def planned(sizes, items):
    rows, cols, depth = sizes
    group = rows * cols
    kinds, shapes, copies = [], [], 0
    for item in items:
        name, array = item[0], item[1]
        shape = array.shape
        if name == "gather":
            assert rows == 4
            second, parts = (item[2:] + (False, 1)[len(item) - 2 :])[:2]
            kinds.append((name, second, parts))
            shape = (shape[0], group) + shape[1:] if second else (group,) + shape
            copies += parts * (4 + 5 * (cols - 1))
        elif name == "shift":
            distances, split = item[2], item[3]
            kinds.append((name, tuple(distances), split))
            shape = (len(distances),) + (shape[1:] if split else shape)
            copies += len(distances)
        elif name == "line":
            parts = item[3] if len(item) > 3 else 1
            kinds.append((name, item[2], parts))
            shape = (depth if item[2] else depth - 1,) + shape
            copies += 2 * (depth - 1) * parts
        else:
            kinds.append((name,))
            if name in ("share", "collect"):
                shape = (group if name == "share" else depth,) + shape
            copies += (depth if name in ("turn", "collect") else group) - 1
        shapes.append(jax.ShapeDtypeStruct(shape, array.dtype))
    sems = [
        pltpu.SemaphoreType.DMA((copies,)),
        pltpu.SemaphoreType.DMA((copies,)),
        pltpu.SemaphoreType.DMA((len(items),)),
    ]
    return tuple(kinds), shapes, sems


class Got:
    def __init__(self, index):
        self.index = index


class Made:
    def __init__(self, index):
        self.index = index


class Stage:
    def __init__(self, body, shapes, *operands, scratch=()):
        self.body, self.shapes, self.operands = body, shapes, operands
        self.scratch = list(scratch)


def exchange(sizes, name, number, *items, before=None, after=None, cover=None, landing=(), shared=()):
    kinds, moved, sems = planned(sizes, items)
    stages = [stage for stage in (before, after) if stage]
    operands = []
    for stage in stages:
        for operand in stage.operands:
            if not isinstance(operand, (Got, Made)):
                operands.append(operand)
    work = list(cover.work) if cover else []
    outs = [s for stage in stages for s in stage.shapes]
    made_shapes = list(cover.shapes) if cover else []
    flown = [i for i in range(len(items)) if i not in landing]
    late = [o.index for o in (after.operands if after else ()) if isinstance(o, Got)]
    late = [i for i in late if i not in landing]
    scratch = []

    def take(shapes):
        first = len(scratch)
        scratch.extend(shapes)
        return slice(first, len(scratch))

    vmem = lambda s: pltpu.VMEM(tuple(s[0]), s[1])
    of = lambda a: (a.shape, a.dtype)
    operand_at = take([vmem(of(a)) for a in operands])
    result_at = take([vmem(s) for s in outs])
    landed_at = take([vmem(of(moved[i])) for i in landing])
    late_at = take([vmem(of(moved[i])) for i in late])
    stage_at = [take(stage.scratch) for stage in stages]
    shared_at = take(list(shared))
    needed = sorted({o.index for o in (after.operands if after else ()) if isinstance(o, Got)})
    others = [i for i in range(len(items)) if i not in needed]
    later = range(1, 2 * sizes[2])
    cover_at = take(cover.scratch) if cover else slice(0, 0)
    copies = len(operands) + len(outs) + len(late)
    copy_at = take([pltpu.SemaphoreType.DMA((max(1, copies),))])
    sems_at = take(sems)

    def body(*refs):
        cuts = [len(operands), len(work), len(items), len(outs), len(made_shapes), len(flown)]
        groups = []
        for cut in cuts:
            groups.append(refs[:cut])
            refs = refs[cut:]
        given, work_refs, sources, results, made_refs, flown_refs = groups
        loaded, held = refs[operand_at], refs[result_at]
        landed, lates, (copy_sem,) = refs[landed_at], refs[late_at], refs[copy_at]
        targets = [None] * len(items)
        for i, ref in zip(flown, flown_refs):
            targets[i] = ref
        for i, ref in zip(landing, landed):
            targets[i] = ref
        moves = Moves(sizes, kinds, sources, targets, refs[sems_at])
        number_of = iter(range(copies))
        copy = lambda a, b: pltpu.make_async_copy(a, b, copy_sem.at[next(number_of)])
        loads = [copy(a, b) for a, b in zip(given, loaded)]
        stores = [copy(a, b) for a, b in zip(held, results)]
        late_loads = [copy(targets[i], b) for i, b in zip(late, lates)]
        split = len([o for o in before.operands if not isinstance(o, Made)]) if before else 0
        first = len(before.shapes) if before else 0
        for load in loads:
            load.start()
        if cover:
            cover.begin(work_refs, refs[cover_at])
        moves.barrier()
        moves.start()
        if before:
            for load in loads[:split]:
                load.wait()
            before.body(*loaded[:split], *held[:first], *refs[stage_at[0]], *refs[shared_at])
            for store in stores[:first]:
                store.start()
        if cover:
            cover.run(work_refs, made_refs, refs[cover_at])
        moves.relay(None, (0,))
        if after:
            moves.relay(needed, later)
            moves.finish(needed)
            for load in late_loads:
                load.start()
            for load in loads[split:]:
                load.wait()
            for load in late_loads:
                load.wait()
            plain = iter(loaded[split:])
            values = []
            for operand in after.operands:
                if isinstance(operand, Made):
                    values.append(held[operand.index])
                elif isinstance(operand, Got) and operand.index in landing:
                    values.append(landed[landing.index(operand.index)])
                elif isinstance(operand, Got):
                    values.append(lates[late.index(operand.index)])
                else:
                    values.append(next(plain))
            after.body(*values, *held[first:], *refs[stage_at[-1]], *refs[shared_at])
            for store in stores[first:]:
                store.start()
        moves.relay(others, later)
        moves.finish(others)
        if cover:
            cover.end(made_refs, refs[cover_at])
        for store in stores:
            store.wait()

    shape = lambda s: jax.ShapeDtypeStruct(tuple(s[0]), s[1])
    return pl.pallas_call(
        body,
        out_shape=tuple(shape(s) for s in outs + made_shapes) + tuple(moved[i] for i in flown),
        in_specs=[HBM] * (len(operands) + len(work) + len(items)),
        out_specs=(HBM,) * (len(outs) + len(made_shapes) + len(flown)),
        scratch_shapes=scratch,
        compiler_params=pltpu.CompilerParams(collective_id=number, has_side_effects=True),
        name=name,
    )(*operands, *work, *[item[1] for item in items])


def dot(a, b, left=1, right=0, precision=None):
    return lax.dot_general(
        a,
        b,
        (((left,), (right,)), ((), ())),
        preferred_element_type=jnp.float32,
        precision=precision,
    )


def widened(source, target):
    size = target.shape[0] // 4

    def piece(i, carry):
        at = pl.ds(pl.multiple_of(i * size, size), size)
        target[at, :] = source[at, :].astype(target.dtype)
        return carry

    lax.fori_loop(0, 4, piece, 0)


def cleared(target):
    size = target.shape[0] // 8

    def piece(i, carry):
        at = pl.ds(pl.multiple_of(i * size, size), size)
        target[at, :] = jnp.zeros((size, target.shape[1]), target.dtype)
        return carry

    lax.fori_loop(0, 8, piece, 0)


def lanes_of(shape):
    return lax.broadcasted_iota(jnp.int32, shape, len(shape) - 1)


def flipped(values):
    lanes = lanes_of(values.shape)
    ahead = pltpu.roll(values, LANES - TURN, 1)
    behind = pltpu.roll(values, TURN, 1)
    return jnp.where(lanes % (2 * TURN) < TURN, ahead, behind)


def beside(blocks_ref):
    return jnp.concatenate([blocks_ref[i] for i in range(blocks_ref.shape[0])], axis=1)


def gain_row(gains_ref):
    return beside(gains_ref).astype(jnp.float32)


def added(blocks):
    return functools.reduce(
        jnp.add, [blocks[i].astype(jnp.float32) for i in range(blocks.shape[0])]
    )


def own_rows(count):
    me = lax.axis_index("row") * lax.axis_size("col") + lax.axis_index("col")
    return pl.ds(pl.multiple_of(me * count, count), count)


def column(row):
    return jnp.broadcast_to(row, (8, row.shape[1])).T[:, 0:1]


def tables_body(cosine, sine):
    step = 64
    lanes = lanes_of((step, LANES))
    power = (lanes % TURN).astype(jnp.float32) * (-math.log(ROPE_BASE) / TURN)
    frequencies = jnp.exp(power)
    base = lax.axis_index("dp") * cosine.shape[0]

    def piece(i, carry):
        at = pl.ds(pl.multiple_of(i * step, step), step)
        positions = base + i * step + lax.broadcasted_iota(jnp.int32, lanes.shape, 0)
        angles = positions.astype(jnp.float32) * frequencies
        cosine[at, :] = jnp.cos(angles)
        value = jnp.sin(angles)
        sine[at, :] = jnp.where(lanes % (2 * TURN) < TURN, -value, value)
        return carry

    lax.fori_loop(0, cosine.shape[0] // step, piece, 0)


def turned(source, target):
    def block(i, carry):
        scaled = RESIDUAL_SCALE * source[i].astype(jnp.float32)
        target[i] = scaled.T.astype(jnp.bfloat16)
        return carry

    lax.fori_loop(0, target.shape[0], block, 0)


def project_body(blocks, gains, w_query, w_pair, cosine, sine, normed, query, pair, own):
    gain = gain_row(gains)
    step = 128

    def piece(i, carry):
        at = pl.ds(pl.multiple_of(i * step, step), step)
        parts = [blocks[k, at, :] for k in range(blocks.shape[0])]
        tokens = jnp.concatenate(parts, axis=1).astype(jnp.float32)
        scale = lax.rsqrt(jnp.mean(tokens * tokens, axis=1, keepdims=True) + EPSILON)
        normed[at, :] = (tokens * scale * gain).astype(jnp.bfloat16)
        return carry

    lax.fori_loop(0, normed.shape[0] // step, piece, 0)
    raw = dot(normed[...], w_query[...])
    query[...] = (raw * cosine[...] + flipped(raw) * sine[...]).astype(jnp.bfloat16)
    raw = dot(normed[...], w_pair[...])
    keys = lanes_of(raw.shape) < LANES // 2
    turned = raw * cosine[...] + flipped(raw) * sine[...]
    pair[...] = jnp.where(keys, turned, raw).astype(jnp.bfloat16)
    for i in range(blocks.shape[0]):
        own[:, i * LANES : (i + 1) * LANES] = blocks[i, own_rows(own.shape[0]), :]


def doubled(pair, keys_ref, values_ref, at):
    wide = pair.astype(jnp.float32)
    other = pltpu.roll(wide, LANES // 2, 1)
    keys = lanes_of(wide.shape) < LANES // 2
    keys_ref[at] = jnp.where(keys, wide, other).astype(jnp.bfloat16)
    values_ref[at] = jnp.where(keys, other, wide).astype(jnp.bfloat16)


def per_head(values):
    first = lanes_of(values.shape) < LANES // 2
    zero = jnp.zeros_like(values)
    return jnp.concatenate(
        [jnp.where(first, values, zero), jnp.where(first, zero, values)], axis=0
    )


def tile_scores(queries, keys_ref, starts, row, block, last, tokens):
    scores = dot(queries, keys_ref[block], 1, 1) * SCORE_SCALE
    at = lanes_of(scores.shape) + block * tokens
    allowed = at >= starts
    if block == last:
        place = row + lax.broadcasted_iota(jnp.int32, scores.shape, 0)
        allowed = allowed & (at <= place + block * tokens)
    return jnp.where(allowed, scores, MASKED)


def doc_row(docs):
    rows = [docs[i : i + 1, :] for i in range(docs.shape[0])]
    return jnp.concatenate(rows, axis=1).astype(jnp.float32)


def attend_tiles(tokens, tile):
    step = 256

    def body(i, carry):
        rows = pl.ds(pl.multiple_of(i * step, step), step)
        tile(rows, lax.rem(i * step, tokens), step)
        return carry

    lax.fori_loop(0, 2 * tokens // step, body, 0)


def attend_first_body(near_grads, far_grads, query, pair, docs, far_docs, own_grad, near_turned, far_turned, start, keys, values, queries, out, tops, totals):
    turned(near_grads, near_turned)
    turned(far_grads, far_turned)
    for i in range(near_grads.shape[0]):
        own_grad[:, i * LANES : (i + 1) * LANES] = near_grads[i, own_rows(own_grad.shape[0]), :]
    tokens = query.shape[0]
    last = keys.shape[0] - 1
    layer = lax.axis_index("dp")
    here = doc_row(docs[...])
    mine = column(here)
    before = jnp.sum((here < mine).astype(jnp.float32), axis=1, keepdims=True)
    for d in range(1, last + 1):
        fewer = (doc_row(far_docs[d - 1]) < mine) | (layer < d)
        before = before + jnp.sum(fewer.astype(jnp.float32), axis=1, keepdims=True)
    start[...] = before.astype(jnp.int32)
    doubled(pair[...], keys, values, last)
    queries[...] = per_head(query[...].astype(jnp.float32)).astype(jnp.bfloat16)

    def tile(rows, row, step):
        starts = start[pl.ds(pl.multiple_of(row, step), step), :]
        scores = tile_scores(queries[rows, :], keys, starts, row, last, last, tokens)
        top = jnp.max(scores, axis=1, keepdims=True)
        terms = jnp.exp(scores - top)
        tops[rows, :] = top
        totals[rows, :] = jnp.sum(terms, axis=1, keepdims=True)
        out[rows, :] = dot(terms.astype(jnp.bfloat16), values[last])

    attend_tiles(tokens, tile)


def attend_rest_body(far, start, mixed, log_total, keys, values, queries, out, tops, totals):
    last, tokens = far.shape[0], far.shape[1]
    for d in range(1, last + 1):
        doubled(far[d - 1], keys, values, last - d)

    def tile(rows, row, step):
        starts = start[pl.ds(pl.multiple_of(row, step), step), :]
        parts = [
            tile_scores(queries[rows, :], keys, starts, row, block, last, tokens)
            for block in range(last)
        ]
        top = functools.reduce(
            jnp.maximum, [jnp.max(part, axis=1, keepdims=True) for part in parts], tops[rows, :]
        )
        parts = [jnp.exp(part - top) for part in parts]
        scale = jnp.exp(tops[rows, :] - top)
        total = functools.reduce(
            jnp.add,
            [jnp.sum(p, axis=1, keepdims=True) for p in parts],
            totals[rows, :] * scale,
        )
        sums = [
            dot(part.astype(jnp.bfloat16), values[block]) for block, part in enumerate(parts)
        ]
        out[rows, :] = functools.reduce(jnp.add, sums, out[rows, :] * scale) / total
        log_total[rows, :] = top + jnp.log(total)

    attend_tiles(tokens, tile)
    first = lanes_of((tokens, LANES)) < LANES // 2
    mixed[...] = jnp.where(first, out[:tokens, :], out[tokens:, :]).astype(jnp.bfloat16)


def attend_again_body(query, pair, far, start, log_total, keys, values, queries, chances):
    tokens = query.shape[0]
    last = far.shape[0]
    doubled(pair[...], keys, values, last)
    for d in range(1, last + 1):
        doubled(far[d - 1], keys, values, last - d)
    queries[...] = per_head(query[...].astype(jnp.float32)).astype(jnp.bfloat16)

    def tile(rows, row, step):
        starts = start[pl.ds(pl.multiple_of(row, step), step), :]
        for block in range(last + 1):
            scores = tile_scores(queries[rows, :], keys, starts, row, block, last, tokens)
            chances[block, rows, :] = jnp.exp(scores - log_total[rows, :])

    attend_tiles(tokens, tile)


def attend_back_body(grad, w_output, mixed, cosine, sine, query_grad, pair_grad, far_grad, output_grad, grads, turned, key_sums, value_sums, keys, values, queries, chances):
    tokens = mixed.shape[0]
    last = keys.shape[0] - 1
    given_grad = grad[...].reshape(tokens, -1)
    grads[...] = per_head(dot(given_grad, w_output[...], 1, 1)).astype(jnp.bfloat16)
    output_sum = dot(mixed[...], given_grad, 0, 0).astype(jnp.bfloat16)
    for i in range(output_grad.shape[0]):
        output_grad[i] = output_sum[:, i * LANES : (i + 1) * LANES]
    for block in range(last + 1):
        cleared(key_sums.at[block])
        cleared(value_sums.at[block])

    def tile(rows, row, step):
        asked, given = queries[rows, :], grads[rows, :]
        products = [dot(given, values[block], 1, 1) for block in range(last + 1)]
        delta = functools.reduce(
            jnp.add,
            [
                jnp.sum(chances[block, rows, :] * product, axis=1, keepdims=True)
                for block, product in enumerate(products)
            ],
        )
        total = jnp.zeros((step, LANES), jnp.float32)
        for block in range(last + 1):
            chance = chances[block, rows, :]
            back = (chance * (products[block] - delta)).astype(jnp.bfloat16)
            total = total + dot(back, keys[block])
            key_sums[block] += dot(back, asked, 0, 0)
            value_sums[block] += dot(chance.astype(jnp.bfloat16), given, 0, 0)
        turned[rows, :] = total

    attend_tiles(tokens, tile)
    first = lanes_of((tokens, LANES)) < LANES // 2
    raw = jnp.where(first, turned[:tokens, :], turned[tokens:, :]) * SCORE_SCALE
    query_grad[...] = (raw * cosine[...] - flipped(raw) * sine[...]).astype(jnp.bfloat16)

    def joined(block):
        by_key, by_value = key_sums[block], value_sums[block]
        by_key = (by_key + pltpu.roll(by_key, LANES // 2, 1)) * SCORE_SCALE
        by_value = by_value + pltpu.roll(by_value, LANES // 2, 1)
        return jnp.where(first, by_key, by_value)

    pair_grad[...] = joined(last)
    for d in range(1, last + 1):
        far_grad[d - 1] = joined(last - d).astype(jnp.bfloat16)


def router_rows(router):
    rows = beside(router).astype(jnp.float32)
    blank = jnp.zeros((LANES - rows.shape[0], rows.shape[1]), jnp.float32)
    return jnp.concatenate([rows, blank], axis=0)


def middle_body(mixed, own, w_output, gains, router, ids_turned, rows, middle, weights, ids_ref):
    experts = router.shape[1]
    width = own.shape[1]
    attn = dot(beside(mixed), w_output[...])
    value = own[...].astype(jnp.float32) + RESIDUAL_SCALE * attn
    middle[...] = value
    scale = lax.rsqrt(jnp.mean(value * value, axis=1, keepdims=True) + EPSILON)
    normed = value * scale * gain_row(gains)
    logits = dot(normed, router_rows(router), 1, 1, precision=HIGH)
    count = own.shape[0]
    ids_ref[...] = ids_turned[...].astype(jnp.float32).T
    ids = ids_ref[own_rows(count), :]
    lanes = lanes_of((count, LANES))
    chosen = jnp.zeros((count, LANES), jnp.float32)
    for k in range(ids.shape[1]):
        chosen = chosen + (ids[:, k : k + 1] == lanes.astype(jnp.float32)).astype(
            jnp.float32
        )
    top = jnp.max(jnp.where(lanes < experts, logits, MASKED), axis=1, keepdims=True)
    terms = jnp.exp(jnp.minimum(logits - top, 0.0)) * chosen
    share = terms / jnp.sum(terms, axis=1, keepdims=True)
    weights[...] = share
    high = share.astype(jnp.bfloat16)
    low = share - high.astype(jnp.float32)
    rows[:, :width] = normed.astype(jnp.bfloat16)
    rows[:, width:] = (high.astype(jnp.float32) + pltpu.roll(low, LANES // 2, 1)).astype(
        jnp.bfloat16
    )


def middle_back_body(back, out_grad, middle, weights, gains, router, middle_grad, attn_grad, logit_grad, gain_part):
    width = middle.shape[1]
    normed_grad = back[0, :, :width].astype(jnp.float32)
    weight_grad = back[0, :, width:].astype(jnp.float32)
    for i in range(1, back.shape[0]):
        normed_grad = normed_grad + back[i, :, :width].astype(jnp.float32)
        weight_grad = weight_grad + back[i, :, width:].astype(jnp.float32)
    share, value = weights[...], middle[...]
    mean = jnp.sum(share * weight_grad, axis=1, keepdims=True)
    logit = share * (weight_grad - mean)
    logit_grad[...] = logit.astype(jnp.bfloat16)
    normed_grad = normed_grad + dot(logit, router_rows(router), precision=HIGH)
    scale = lax.rsqrt(jnp.mean(value * value, axis=1, keepdims=True) + EPSILON)
    gain_part[...] = jnp.sum(normed_grad * value * scale, axis=0, keepdims=True)
    scaled = normed_grad * gain_row(gains)
    norm_dot = jnp.sum(scaled * value, axis=1, keepdims=True)
    total = (
        out_grad[...].astype(jnp.float32)
        + scale * scaled
        - value * (scale * scale * scale * norm_dot / width)
    )
    middle_grad[...] = total
    attn_grad[...] = (RESIDUAL_SCALE * total).astype(jnp.bfloat16)


def project_back_body(query_grad, pair_grad, returned, normed, w_query, w_pair, cosine, sine, output_turned, logit, rows, gains, gain_moe, partial, sums, output_first, output_last, gain_parts):
    layer = lax.axis_index("dp")
    depth = lax.axis_size("dp")
    total = pair_grad[...]
    for i in range(returned.shape[0]):
        total = total + jnp.where(
            layer + i + 1 < depth, returned[i].astype(jnp.float32), 0.0
        )
    keys = lanes_of(total.shape) < LANES // 2
    turned = total * cosine[...] - flipped(total) * sine[...]
    pair_low = jnp.where(keys, turned, total).astype(jnp.bfloat16)
    query_low = query_grad[...]
    whole = dot(query_low, w_query[...], 1, 1) + dot(pair_low, w_pair[...], 1, 1)
    partial[...] = whole.astype(jnp.bfloat16)
    gain_attn = jnp.sum(whole * normed[...].astype(jnp.float32), axis=0, keepdims=True)
    gain_attn = gain_attn / gain_row(gains)
    gain_parts[...] = jnp.zeros_like(gain_parts)
    for i in range(gain_parts.shape[0]):
        at = slice(i * LANES, (i + 1) * LANES)
        gain_parts[i, 0:1, :] = gain_attn[:, at]
        gain_parts[i, 1:2, :] = gain_moe[0:1, at]
    width = normed.shape[1]
    sums[:width, :] = dot(normed[...], query_low, 0, 0).astype(jnp.bfloat16)
    sums[width : 2 * width, :] = dot(normed[...], pair_low, 0, 0).astype(jnp.bfloat16)
    output_sum = added(output_turned).astype(jnp.bfloat16)
    output_first[...] = output_sum[: output_first.shape[0], :]
    output_last[...] = output_sum[output_first.shape[0] :, :]
    mine = rows[:, own_rows(LANES)]
    named = logit[...].reshape(normed.shape[0], LANES)
    sums[2 * width : 2 * width + LANES, :] = dot(named, mine, 0, 0).astype(jnp.bfloat16)


def results_body(blocks, moe, own, middle, middle_grad, gains, gain_blocks, turned, block_out, in_grad, gain_sum, summed):
    gain_sum[...] = added(gain_blocks)
    summed[...] = added(turned).astype(jnp.bfloat16)
    width = own.shape[1]
    normed_grad = blocks[0].astype(jnp.float32)
    branch = moe[0].astype(jnp.float32)
    for i in range(1, blocks.shape[0]):
        normed_grad = normed_grad + blocks[i].astype(jnp.float32)
        branch = branch + moe[i].astype(jnp.float32)
    value = own[...].astype(jnp.float32)
    scale = lax.rsqrt(jnp.mean(value * value, axis=1, keepdims=True) + EPSILON)
    scaled = normed_grad * gain_row(gains)
    norm_dot = jnp.sum(scaled * value, axis=1, keepdims=True)
    grad = (
        middle_grad[...] + scale * scaled - value * (scale * scale * scale * norm_dot / width)
    ).astype(jnp.bfloat16)
    out = (middle[...] + RESIDUAL_SCALE * branch).astype(jnp.bfloat16)
    for i in range(block_out.shape[0]):
        at = slice(i * LANES, (i + 1) * LANES)
        block_out[i] = out[:, at]
        in_grad[i] = grad[:, at]


def expert_terms(gate_up, active_grad, weight):
    hidden = active_grad.shape[0]
    gate, up = gate_up[:hidden], gate_up[hidden:]
    sigmoid = jax.nn.sigmoid(gate)
    silu = gate * sigmoid
    ungated = silu * up
    active = (ungated * weight).astype(jnp.bfloat16)
    scaled = active_grad * weight
    gate_grad = (scaled * up * sigmoid * (1.0 + gate * (1.0 - sigmoid))).astype(jnp.bfloat16)
    up_grad = (scaled * silu).astype(jnp.bfloat16)
    return active, jnp.concatenate([gate_grad, up_grad], axis=0), active_grad * ungated


def weight_rows(extra):
    turned = extra.astype(jnp.float32).T
    return turned[: LANES // 2] + turned[LANES // 2 :]


def local_experts_body(sizes, kinds, rows_ref, grads_ref, in_ref, out_ref, sent_grads, sent_rows, moe_ref, back_ref, flat_ref, in_sum, out_sum, got_grads, got_rows, moe_acc, back_acc, share, weights, spread, *sems):
    step, steps = pl.program_id(0), pl.num_programs(0)
    each, hidden, width = out_ref.shape
    parts = hidden // LANES
    moves = Moves(sizes, kinds, [sent_grads, sent_rows], [got_grads, got_rows], sems)

    @pl.when(step == 0)
    def _():
        moves.barrier()
        moves.start([0])
        cleared(moe_acc)
        cleared(back_acc)
        share[...] = jnp.zeros_like(share)
        weights[...] = weight_rows(rows_ref[:, width:])

    @pl.when(step == 2 * steps // 8)
    def _():
        moves.start([1])

    for when, item, stage in ((3, 0, 0), (6, 1, 0), (7, 0, 1)):

        @pl.when(step == when * steps // 8)
        def _(item=item, stage=stage):
            moves.relay([item], (stage,))

    for i in range(each):
        spread[i] = in_ref[i].astype(jnp.float32)
        for part in range(parts):
            for half in range(2):
                at = half * hidden + part * LANES
                flat_ref[i, :, at : at + LANES] = spread[
                    i, pl.ds(part * 2 + half, width, stride=2 * parts), :
                ].astype(jnp.bfloat16)
        expert = (lax.axis_index("row") * steps + step) * each + i
        active, gate_up_grad, shares = expert_terms(
            dot(flat_ref[i], rows_ref[:, :width], 0, 1),
            dot(out_ref[i], grads_ref[...]),
            weights[pl.ds(expert, 1), :],
        )
        share[pl.ds(expert, 1), :] = jnp.sum(shares, axis=0, keepdims=True)
        moe_acc[...] += dot(active, out_ref[i], 0, 0)
        back_acc[...] += dot(gate_up_grad, flat_ref[i], 0, 1)
        in_sum[i] = dot(gate_up_grad, rows_ref[:, :width]).astype(jnp.bfloat16)
        out_sum[i] = dot(active, grads_ref[...], 1, 1).astype(jnp.bfloat16)

    @pl.when(step == steps - 1)
    def _():
        widened(moe_acc, moe_ref)
        widened(back_acc, back_ref.at[:, :width])
        back_ref[:, width:] = share[...].T.astype(jnp.bfloat16)
        moves.relay([1], (1,))
        moves.finish()


def local_experts(sizes, number, rows, grads, w_in, w_out, sent_grads, sent_rows):
    tokens, wide = rows.shape
    experts, hidden, width = w_out.shape
    each = 1
    low = jnp.bfloat16
    kinds, shapes, sems = planned(
        sizes,
        [
            ("gather", sent_grads, True, sent_grads.shape[0]),
            ("gather", sent_rows, True, sent_rows.shape[0]),
        ],
    )
    whole = lambda s: pl.BlockSpec(s, lambda e: (0,) * len(s))
    some = lambda s: pl.BlockSpec((each,) + s[1:], lambda e: (e,) + (0,) * (len(s) - 1))
    outs = [
        (tokens, width),
        (tokens, wide),
        (experts, width, 2 * hidden),
        (experts, 2 * hidden, width),
        (experts, hidden, width),
    ]
    return pl.pallas_call(
        functools.partial(local_experts_body, sizes, kinds),
        grid=(experts // each,),
        in_specs=[
            whole(rows.shape),
            whole(grads.shape),
            some(w_in.shape),
            some(w_out.shape),
            HBM,
            HBM,
        ],
        out_specs=(whole(outs[0]), whole(outs[1]), *[some(s) for s in outs[2:]], HBM, HBM),
        out_shape=tuple(jax.ShapeDtypeStruct(s, low) for s in outs) + tuple(shapes),
        scratch_shapes=[
            pltpu.VMEM((tokens, width), jnp.float32),
            pltpu.VMEM((tokens, width), jnp.float32),
            pltpu.VMEM((LANES, tokens), jnp.float32),
            pltpu.VMEM((LANES // 2, tokens), jnp.float32),
            pltpu.VMEM((each,) + w_in.shape[1:], jnp.float32),
        ]
        + sems,
        compiler_params=pltpu.CompilerParams(collective_id=number, has_side_effects=True),
        name="local_experts",
    )(rows, grads, w_in, w_out, sent_grads, sent_rows)


class Sums:
    def __init__(self, rows, grads, weights, turned, load_sem, *sums):
        self.rows, self.grads, self.weights = rows, grads, weights
        self.turned, self.load_sem, self.sums = turned, load_sem, sums

    def load(self, which, source):
        target = (self.rows, self.grads)[which]
        return pltpu.make_async_copy(source, target, self.load_sem.at[which])

    def ready(self):
        layers, width, tokens = self.grads.shape

        def block(i, carry):
            at = pl.ds(pl.multiple_of(i * tokens, tokens), tokens)
            self.weights[i] = weight_rows(self.rows[at, width:])
            return carry

        lax.fori_loop(0, layers, block, 0)

    def make(self, index, w_in, w_out, in_part, out_part, made, arrive):
        layers, width, tokens = self.grads.shape
        hidden = w_out.shape[0]
        arrive(0)
        if self.sums:
            arrive(1)
        later = arrive

        def part_of(at, pieces, arrive=lambda i: None if self.sums else later(i)):
            first = at * tokens if isinstance(at, int) else pl.multiple_of(at * tokens, tokens)
            block = self.rows[pl.ds(first, pieces * tokens), :width]
            gate_up = dot(w_in[...], block, 0, 1)
            arrive(1)
            weight = jnp.concatenate(
                [self.weights[at + i, pl.ds(index, 1), :] for i in range(pieces)], axis=1
            )
            active_grad = jnp.concatenate(
                [dot(w_out[...], self.grads[at + i]) for i in range(pieces)], axis=1
            )
            active, gate_up_grad, _ = expert_terms(gate_up, active_grad, weight)
            out_total = functools.reduce(
                jnp.add,
                [
                    dot(active[:, i * tokens : (i + 1) * tokens], self.grads[at + i], 1, 1)
                    for i in range(pieces)
                ],
            )
            return dot(gate_up_grad, block), out_total

        if not self.sums:
            in_total, out_total = part_of(0, layers)
        else:
            whole, out_acc = self.sums
            whole[...] = jnp.zeros_like(whole)
            out_acc[...] = jnp.zeros_like(out_acc)

            def more(i, carry):
                in_more, out_more = part_of(i, 1)
                whole[...] += in_more
                out_acc[...] += out_more
                return carry

            lax.fori_loop(0, layers, more, 0)
            in_total, out_total = whole[...], out_acc[...]
        arrive(2)
        in_total = in_total + in_part[...].astype(jnp.float32)
        parts = hidden // LANES
        for part in range(parts):
            for half in range(2):
                at = half * hidden + part * LANES
                self.turned[pl.ds(part * 2 + half, width, stride=2 * parts), :] = in_total[
                    at : at + LANES, :
                ].T
        made[...] = self.turned[...].astype(jnp.bfloat16)
        return out_total + out_part[...].astype(jnp.float32)


def sums_scratch(layers, tokens, width, hidden):
    low, full = jnp.bfloat16, jnp.float32
    return [
        pltpu.VMEM((layers * tokens, width + LANES), low),
        pltpu.VMEM((layers, width, tokens), low),
        pltpu.VMEM((layers, LANES // 2, tokens), full),
        pltpu.VMEM((width * 2 * hidden // LANES, LANES), full),
        pltpu.SemaphoreType.DMA((2,)),
    ] + [pltpu.VMEM((k * hidden, width), full) for k in (2, 1) if layers > 4]


class Cover:
    def __init__(self, first, many, work):
        w_in, w_out, in_part, out_part, rows_far, grads_far = work
        layers, width, tokens = grads_far.shape
        self.experts, hidden, _ = w_out.shape
        self.first, self.many, self.work = first, many, work
        low = jnp.bfloat16
        self.shapes = [
            ((many, width * 2 * hidden // LANES, LANES), low),
            ((many, hidden, width), low),
        ]
        self.scratch = [pltpu.VMEM((many,) + a.shape[1:], low) for a in work[:4]]
        self.scratch += [pltpu.VMEM(*s) for s in self.shapes]
        self.scratch += [pltpu.SemaphoreType.DMA((4, many)), pltpu.SemaphoreType.DMA((2, many))]
        self.scratch += sums_scratch(layers, tokens, width, hidden)

    def load(self, which, i, work, refs):
        source, sem = work[which].at[self.first + i], refs[6].at[which, i]
        return pltpu.make_async_copy(source, refs[which].at[i], sem)

    def begin(self, work, refs):
        sums = Sums(*refs[8:])
        sums.load(0, work[4]).start()
        self.load(0, 0, work, refs).start()
        sums.load(1, work[5]).start()
        for which in (1, 2, 3):
            self.load(which, 0, work, refs).start()
        for i in range(1, self.many):
            for which in range(4):
                self.load(which, i, work, refs).start()

    def stores(self, i, made, refs):
        return [
            pltpu.make_async_copy(refs[4 + k].at[i], made[k].at[i], refs[7].at[k, i])
            for k in range(2)
        ]

    def run(self, work, made, refs):
        sums = Sums(*refs[8:])

        def expert(i, carry):
            def arrive(point):
                @pl.when(i == 0)
                def _():
                    if point == 0:
                        sums.load(0, work[4]).wait()
                        sums.ready()
                    if point == 1:
                        sums.load(1, work[5]).wait()

                for which in ((0,), (1,), (2, 3))[point]:
                    self.load(which, i, work, refs).wait()

            index = lax.axis_index("row") * self.experts + self.first + i
            out_total = sums.make(index, *[refs[k].at[i] for k in range(5)], arrive)
            refs[5][i] = out_total.astype(jnp.bfloat16)
            for store in self.stores(i, made, refs):
                store.start()
            return carry

        lax.fori_loop(0, self.many, expert, 0)

    def end(self, made, refs):
        for i in range(self.many):
            for store in self.stores(i, made, refs):
                store.wait()


def outputs_body(count, total, *refs):
    pieces = total // count
    sums, smalls = refs[: 2 * pieces], refs[2 * pieces : 2 * pieces + 6]
    gin, gout, *others = refs[2 * pieces + 6 : 2 * pieces + 16]
    block_out, in_grad, gain_attn, gain_moe, query, pair, output, router = others
    in_low, out_low, in_full, out_full, load_sem, store_sem = refs[2 * pieces + 16 :]
    ring = in_full.shape[0]

    def load(k, i):
        low = (in_low, out_low)[k]
        source = sums[k * pieces + i // count].at[i % count]
        return pltpu.make_async_copy(source, low.at[i], load_sem.at[k, i])

    def store(k, i):
        held, target = ((in_full, gin), (out_full, gout))[k]
        return pltpu.make_async_copy(held.at[i % ring], target.at[i], store_sem.at[k, i % ring])

    for i in range(total):
        for k in range(2):
            load(k, i).start()
    blocks, in_blocks, gains, summed, output_first, output_last = smalls
    width = gout.shape[2]
    for i in range(blocks.shape[0]):
        at = pl.ds(i * blocks.shape[1], blocks.shape[1])
        block_out[at, :] = blocks[i]
        in_grad[at, :] = in_blocks[i]
    gain_sum = jnp.sum(gains[...], axis=0)
    gain_attn[...] = gain_sum[0:1, :]
    gain_moe[...] = gain_sum[1:2, :]
    query[...] = summed[:width, :].astype(jnp.float32)
    pair[...] = summed[width : 2 * width, :].astype(jnp.float32)
    router[...] = summed[2 * width : 2 * width + router.shape[0], :].astype(jnp.float32)
    half = output_first.shape[1]
    for i in range(width // half):
        from_first = i % 2 == 0
        rows = (output_first if from_first else output_last)[i // 2].astype(jnp.float32)
        for j in range(max(1, half // LANES)):
            place = i * half + j * LANES
            at = place // LANES
            part = rows[j * LANES : (j + 1) * LANES, :]
            first = place % LANES
            output[first : first + part.shape[0], at * LANES : (at + 1) * LANES] = part
    for i in range(total):
        for k in range(2):
            load(k, i).wait()
            if i >= ring:
                store(k, i - ring).wait()
        for low, held in ((in_low, in_full), (out_low, out_full)):
            widened(low.at[i], held.at[i % ring])
        for k in range(2):
            store(k, i).start()
    for i in range(total - ring, total):
        for k in range(2):
            store(k, i).wait()


def outputs(in_sums, out_sums, hidden, experts, *smalls):
    count = in_sums[0].shape[0]
    total = count * len(in_sums)
    width = out_sums[0].shape[2]
    parts = hidden // LANES
    lanes = smalls[0].shape[2]
    tokens = smalls[0].shape[0] * smalls[0].shape[1]
    low, full = jnp.bfloat16, jnp.float32
    large = [(width * 2 * parts, LANES), (hidden, width)]
    shapes = [((total,) + s, full) for s in large] + [
        ((tokens, lanes), low),
        ((tokens, lanes), low),
        ((1, LANES), full),
        ((1, LANES), full),
        ((width, LANES), full),
        ((width, LANES), full),
        ((LANES, width), full),
        ((experts, LANES), full),
    ]
    ring = min(4, total)
    gin, *others = pl.pallas_call(
        functools.partial(outputs_body, count, total),
        in_specs=[HBM] * (2 * len(in_sums)) + [FULL] * len(smalls),
        out_specs=(HBM, HBM) + (FULL,) * (len(shapes) - 2),
        out_shape=tuple(jax.ShapeDtypeStruct(*shape) for shape in shapes),
        scratch_shapes=[pltpu.VMEM((total,) + s, low) for s in large]
        + [pltpu.VMEM((ring,) + s, full) for s in large]
        + [pltpu.SemaphoreType.DMA((2, total)), pltpu.SemaphoreType.DMA((2, ring))],
        name="outputs",
    )(*in_sums, *out_sums, *smalls)
    gin = gin.reshape(total, width, parts, 2, LANES).transpose(0, 1, 3, 2, 4)
    return gin.reshape(total, width, 2, hidden), *others


def local(
    sizes,
    tokens,
    out_grad,
    doc_ids,
    expert_ids,
    gain_attn,
    w_query,
    w_key_value,
    w_output,
    gain_moe,
    w_router,
    w_expert_in,
    w_expert_out,
):
    rows, cols, depth = sizes
    group = rows * cols
    tok_rows, feat_local = tokens.shape
    width = w_query.shape[0]
    experts = w_router.shape[1]
    expert_local, hidden = w_expert_out.shape[0], w_expert_out.shape[1]
    longest_doc = min(LONGEST, tok_rows * depth // 2)
    hop_count = longest_doc // tok_rows
    own = tok_rows // group
    low, full = jnp.bfloat16, jnp.float32
    layer = lax.axis_index("dp")
    me = lax.axis_index("row") * cols + lax.axis_index("col")
    everyone = list(range(1, depth))
    hops = list(range(1, hop_count + 1))

    w_pair = w_key_value.reshape(width, -1)
    block = (tok_rows, LANES)
    cosine, sine, normed, query, pair, tokens_own, gains, gains_moe, router, docs_far, grads_shifted, grad_blocks = exchange(
        sizes,
        "gather_tokens",
        0,
        ("gather", tokens, False, 2),
        ("share", gain_attn.reshape(1, LANES)),
        ("share", gain_moe.reshape(1, LANES)),
        ("share", w_router.T),
        ("shift", doc_ids.reshape(-1, LANES), everyone, False),
        ("shift", out_grad, everyone, False),
        ("gather", out_grad, False, 2),
        before=Stage(tables_body, [(block, full), (block, full)]),
        after=Stage(
            project_body,
            [((tok_rows, width), low), (block, low), (block, low), ((own, width), low)],
            Got(0),
            Got(1),
            w_query,
            w_pair,
            Made(0),
            Made(1),
        ),
        landing=(0,),
    )

    stack = (hop_count + 1,) + block
    twice = (2 * tok_rows, LANES)
    turned_block = (LANES, tok_rows)
    whole = (2 * tok_rows, 1)
    grad_own, grads_near, far_turned, start, mixed, log_total, far, output_blocks = exchange(
        sizes,
        "shift_pairs",
        1,
        ("shift", pair, hops, False),
        ("gather", w_output, False, 4),
        before=Stage(
            attend_first_body,
            [
                ((own, width), low),
                ((group,) + turned_block, low),
                ((depth - 1,) + turned_block, low),
                ((tok_rows, 1), jnp.int32),
            ],
            grad_blocks,
            grads_shifted,
            query,
            pair,
            doc_ids.reshape(-1, LANES),
            docs_far,
        ),
        after=Stage(
            attend_rest_body,
            [(block, low), (whole, full)],
            Got(0),
            Made(3),
        ),
        shared=[
            pltpu.VMEM(stack, low),
            pltpu.VMEM(stack, low),
            pltpu.VMEM(twice, low),
            pltpu.VMEM(twice, full),
            pltpu.VMEM(whole, full),
            pltpu.VMEM(whole, full),
        ],
    )
    output_full = output_blocks.reshape(-1, width)

    rows_own, middle, weights = exchange(
        sizes,
        "swap_mixed",
        2,
        ("swap", mixed.reshape(group, own, LANES)),
        after=Stage(
            middle_body,
            [((own, width + LANES), low), ((own, width), full), ((own, LANES), full)],
            Got(0),
            tokens_own,
            output_full,
            gains_moe,
            router,
            expert_ids.T,
            scratch=[pltpu.VMEM(expert_ids.shape, full)],
        ),
        landing=(0,),
    )
    rows_blocks, rows_shifted = exchange(
        sizes,
        "gather_rows",
        3,
        ("gather", rows_own, False, 2),
        ("line", rows_own, False, 2),
    )
    rows_near = rows_blocks.reshape(tok_rows, -1)
    parts = hidden // LANES
    in_rows = w_expert_in.reshape(expert_local, width, 2, parts, LANES)
    in_rows = in_rows.transpose(0, 1, 3, 2, 4).reshape(expert_local, -1, LANES)
    moe_partial, back_partial, in_flat, in_part, out_part, grads_far, rows_far = local_experts(
        sizes,
        9,
        rows_near,
        grads_near.reshape(width, tok_rows),
        in_rows,
        w_expert_out,
        far_turned,
        rows_shifted,
    )
    rows_far = rows_far.reshape((depth - 1) * tok_rows, -1)
    grads_far = grads_far.reshape(depth - 1, width, tok_rows)
    work = (in_flat, w_expert_out, in_part, out_part, rows_far, grads_far)
    share = expert_local // 4
    unit = 16 * depth
    in_sums, out_sums = [], []

    def beneath(name, number, *items, after=None, landing=()):
        cover = Cover(len(in_sums) * share, share, work)
        in_sum, out_sum, *moved = exchange(
            sizes, name, number, *items, after=after, cover=cover, landing=landing
        )
        if after:
            count = len(after.shapes)
            results = [in_sum, out_sum, *moved]
            in_sum, out_sum = results[count], results[count + 1]
            moved = results[:count] + results[count + 2 :]
        in_sums.append(in_sum)
        out_sums.append(out_sum)
        return moved

    middle_grad, attn_grad, logit_grad, gain_moe_part = beneath(
        "swap_back",
        4,
        ("swap", back_partial.reshape(group, own, -1)),
        after=Stage(
            middle_back_body,
            [
                ((own, width), full),
                ((own, width), low),
                ((own, LANES), low),
                ((1, width), full),
            ],
            Got(0),
            grad_own,
            middle,
            weights,
            gains_moe,
            router,
        ),
        landing=(0,),
    )
    query_grad, pair_grad, far_grad, output_sum, logit_blocks = exchange(
        sizes,
        "gather_attn_grad",
        5,
        ("gather", attn_grad, False, 2),
        ("gather", logit_grad),
        before=Stage(attend_again_body, [], query, pair, far, start, log_total),
        after=Stage(
            attend_back_body,
            [
                (block, low),
                (block, full),
                ((hop_count,) + block, low),
                ((group, LANES, LANES), low),
            ],
            Got(0),
            w_output,
            mixed,
            cosine,
            sine,
            scratch=[
                pltpu.VMEM(twice, low),
                pltpu.VMEM(twice, full),
                pltpu.VMEM(stack, full),
                pltpu.VMEM(stack, full),
            ],
        ),
        landing=(0,),
        shared=[
            pltpu.VMEM(stack, low),
            pltpu.VMEM(stack, low),
            pltpu.VMEM(twice, low),
            pltpu.VMEM((hop_count + 1, 2 * tok_rows, tok_rows), full),
        ],
    )
    length = (2 * width + LANES + unit - 1) // unit * unit
    partial, sums, output_first, output_last, gain_parts, moe_blocks = beneath(
        "shift_grads",
        6,
        ("shift", far_grad, [-d for d in hops], True),
        ("swap", moe_partial.reshape(group, own, width)),
        ("turn", output_sum.reshape(depth, width // depth, LANES)),
        after=Stage(
            project_back_body,
            [
                ((tok_rows, width), low),
                ((length, LANES), low),
                ((width // depth // 2, LANES), low),
                ((width // depth // 2, LANES), low),
                ((group, 8, LANES), full),
            ],
            query_grad,
            pair_grad,
            Got(0),
            normed,
            w_query,
            w_pair,
            cosine,
            sine,
            Got(2),
            logit_blocks,
            rows_near,
            gains,
            gain_moe_part,
        ),
        landing=(0, 2),
    )
    pieces = (group, own, LANES)
    block_out, in_grad, gain_sum, summed, output_first = beneath(
        "swap_partial",
        7,
        ("swap", partial.reshape(group, own, width)),
        ("turn", sums.reshape(depth, length // depth, LANES)),
        ("swap", gain_parts),
        ("collect", output_first),
        after=Stage(
            results_body,
            [(pieces, low), (pieces, low), ((8, LANES), full), ((length // depth, LANES), low)],
            Got(0),
            moe_blocks,
            tokens_own,
            middle,
            middle_grad,
            gains,
            Got(2),
            Got(1),
        ),
        landing=(0, 1, 2),
    )
    block_out, in_grad, sums, output_last, gain_all = beneath(
        "swap_results",
        8,
        ("swap", block_out),
        ("swap", in_grad),
        ("collect", summed),
        ("collect", output_last),
        ("collect", gain_sum),
    )
    grad_in, grad_out, block_out, in_grad, gain_attn_sum, gain_moe_sum, query_sum, pair_sum, output_sum, router_sum = outputs(
        in_sums,
        out_sums,
        hidden,
        experts,
        block_out,
        in_grad,
        gain_all,
        sums.reshape(length, LANES),
        output_first,
        output_last,
    )
    return (
        block_out,
        in_grad,
        gain_attn_sum.reshape(LANES),
        query_sum,
        pair_sum.reshape(w_key_value.shape),
        output_sum,
        gain_moe_sum.reshape(LANES),
        router_sum.T,
        grad_in,
        grad_out,
    )


def solution(mesh):
    in_specs = (
        P("dp", ("row", "col")),
        P("dp", ("row", "col")),
        P("dp"),
        P("dp", None),
        P(("row", "col")),
        P(None, ("row", "col")),
        P(None, ("row", "col"), None),
        P(("row", "col"), None),
        P(("row", "col")),
        P(("row", "col"), None),
        P("row", None, None, "col"),
        P("row", "col", None),
    )
    out_specs = (
        P("dp", ("row", "col")),
        P("dp", ("row", "col")),
        P(("row", "col")),
        P(None, ("row", "col")),
        P(None, ("row", "col"), None),
        P(("row", "col"), None),
        P(("row", "col")),
        P(("row", "col"), None),
        P("row", None, None, "col"),
        P("row", "col", None),
    )
    sizes = (mesh.shape["row"], mesh.shape["col"], mesh.shape["dp"])
    return jax.shard_map(
        functools.partial(local, sizes),
        mesh=mesh,
        in_specs=in_specs,
        out_specs=out_specs,
        check_vma=False,
    )
```

profile of v0, /device:TPU:0, one launch (start us, length us, event | category | flops | bytes accessed | tf_op | source)
XLA Modules:
  0.0 213.7 jit_solution(66595027223455586)
XLA Ops:
  0.6 23.6 %gather_tokens.1 = (f32[512,128]{1,0:T(8,128)}, f32[512,128]{1,0:T(8,128)}, bf16[512,1024]{1,0:T(8,128)(2,1)}, bf16[512,128]{1,0:T(8,128)(2,1)}, bf16[512,128]{1...) custom-call(bf16[1024,128]{1,0:T(8,128)(2,1)} %refs_3_.1, ...), custom_call_target="tpu_custom_call" | custom-call | tf_op jit(solution)/shard_map/gather_tokens/pallas_call | solution.py:415
  24.2 18.9 %shift_pairs.1 = (bf16[64,1024]{1,0:T(8,128)(2,1)}, bf16[8,128,512]{2,1,0:T(8,128)(2,1)}, bf16[3,128,512]{2,1,0:T(8,128)(2,1)}, s32[512,1]{1,0:T(8,128)}, bf16[5...) custom-call(bf16[8,512,128]{2,1,0:T(8,128)(2,1)} %get-tuple-element.85.ref, ...), custom_call_target="tpu_custom_call" | custom-call | tf_op jit(solution)/shard_map/shift_pairs/pallas_call | solution.py:415
  43.2 7.6 %swap_mixed.1 = (bf16[64,1152]{1,0:T(8,128)(2,1)}, f32[64,1024]{1,0:T(8,128)}, f32[64,128]{1,0:T(8,128)}) custom-call(bf16[64,1024]{1,0:T(8,128)(2,1)} %get-tuple-element.91.refs_0_.refs_1_, bf16[1024,1024]{1,0:T(8,128)(2,1)} %bitcast.45, bf16[8,1,128]{2,1,0:T(2,128)(2,1)} %get-tuple-element.93.refs_2_.refs_3_, ...), custom_call_target="tpu_custom_call" | custom-call | tf_op jit(solution)/shard_map/swap_mixed/pallas_call | solution.py:415
  50.8 14.5 %gather_rows.1 = (bf16[8,64,1152]{2,1,0:T(8,128)(2,1)}, bf16[3,64,1152]{2,1,0:T(8,128)(2,1)}) custom-call(bf16[64,1152]{1,0:T(8,128)(2,1)} %get-tuple-element.98.refs_0_.refs_1_, bf16[64,1152]{1,0:T(8,128)(2,1)} %get-tuple-element.98.refs_0_.refs_1_), custom_call_target="tpu_custom_call" | custom-call | tf_op jit(solution)/shard_map/gather_rows/pallas_call | solution.py:415
  65.3 36.9 %local_experts.1 = (bf16[512,1024]{1,0:T(8,128)(2,1)}, bf16[512,1152]{1,0:T(8,128)(2,1)}, bf16[8,1024,512]{2,1,0:T(8,128)(2,1)}, bf16[8,512,1024]{2,1,0:T(8,128)...) custom-call(bf16[512,1152]{1,0:T(8,128)(2,1)} %bitcast.43, ...), custom_call_target="tpu_custom_call" | custom-call | tf_op jit(solution)/shard_map/local_experts/pallas_call | solution.py:920
  102.1 17.9 %swap_back.1 = (f32[64,1024]{1,0:T(8,128)}, bf16[64,1024]{1,0:T(8,128)(2,1)}, bf16[64,128]{1,0:T(8,128)(2,1)}, f32[1,1024]{1,0:T(1,128)}, bf16[2,4096,128]{2,1,0:T(8,128)(2,1)}, /*index=5*/bf16[2,256,1024]{2,1,0:T(8,128)(2,1)}) custom-call(bf16[64,1024]{1,0:T(8,128)(2,1)} %get-tuple-element.90.refs_0_, f32[64,1024]{1,0:T(8,128)} %get-tuple-element.96.refs_1_.refs_2_, ...), custom_call_target="tpu_custom_call" | custom-call | tf_op jit(solution)/shard_map/swap_back/pallas_call | solution.py:415
  120.1 19.5 %gather_attn_grad.1 = (bf16[512,128]{1,0:T(8,128)(2,1)}, f32[512,128]{1,0:T(8,128)}, bf16[2,512,128]{2,1,0:T(8,128)(2,1)}, bf16[8,128,128]{2,1,0:T(8,128)(2,1)}, bf16[8,64,128]{2,1,0:T(8,128)(2,1)}) custom-call(bf16[512,128]{1,0:T(8,128)(2,1)} %get-tuple-element.87.refs_2_.refs_0_, bf16[512,128]{1,0:T(8,128)(2,1)} %get-tuple-element.88.refs_3_.refs_6_.refs_1_, ...), custom_call_target="tpu_custom_call" | custom-call | tf_op jit(solution)/shard_map/gather_attn_grad/pallas_call | solution.py:415
  139.6 20.1 %shift_grads.1 = (bf16[512,1024]{1,0:T(8,128)(2,1)}, bf16[2176,128]{1,0:T(8,128)(2,1)}, bf16[128,128]{1,0:T(8,128)(2,1)}, bf16[128,128]{1,0:T(8,128)(2,1)}, f32[...) custom-call(bf16[512,128]{1,0:T(8,128)(2,1)} %get-tuple-element.117., ...), custom_call_target="tpu_custom_call" | custom-call | tf_op jit(solution)/shard_map/shift_grads/pallas_call | solution.py:415
  159.7 19.4 %swap_partial.1 = (bf16[8,64,128]{2,1,0:T(8,128)(2,1)}, bf16[8,64,128]{2,1,0:T(8,128)(2,1)}, f32[8,128]{1,0:T(8,128)}, bf16[544,128]{1,0:T(8,128)(2,1)}, bf16[2,...) custom-call(bf16[8,64,1024]{2,1,0:T(8,128)(2,1)} %get-tuple-element.127.refs_0_, ...), custom_call_target="tpu_custom_call" | custom-call | tf_op jit(solution)/shard_map/swap_partial/pallas_call | solution.py:415
  179.1 19.8 %swap_results.1 = (bf16[2,4096,128]{2,1,0:T(8,128)(2,1)}, bf16[2,256,1024]{2,1,0:T(8,128)(2,1)}, bf16[8,64,128]{2,1,0:T(8,128)(2,1)}, bf16[8,64,128]{2,1,0:T(8,1...) custom-call(bf16[8,1024,512]{2,1,0:T(8,128)(2,1)} %get-tuple-element.103.refs_5_.refs_11_, ...), custom_call_target="tpu_custom_call" | custom-call | tf_op jit(solution)/shard_map/swap_results/pallas_call | solution.py:415
  198.9 14.5 %outputs.1 = (f32[8,4096,128]{2,1,0:T(8,128)}, f32[8,256,1024]{2,1,0:T(8,128)}, bf16[512,128]{1,0:T(8,128)(2,1)}, bf16[512,128]{1,0:T(8,128)(2,1)}, f32[1,128]{1...) custom-call(bf16[2,4096,128]{2,1,0:T(8,128)(2,1)} %get-tuple-element, ...), custom_call_target="tpu_custom_call" | custom-call | tf_op jit(solution)/shard_map/outputs/pallas_call | solution.py:1177
where the time goes:
time: 214 us
  Pallas kernels  213 us (100%)
    pallas_call x9, Pallas kernels, exchange(): pl.pallas_call(body, out_shape=tuple((shape(s) for s in outs + made_shape...  161 us
    pallas_call x1, Pallas kernels, local_experts(): pl.pallas_call(functools.partial(local_experts_body, sizes, kinds), grid=...  36.9 us
    pallas_call x1, Pallas kernels, outputs(): pl.pallas_call(functools.partial(outputs_body, count, total), in_specs=[H...  14.5 us

commit v1 on v0

--- a/solution.py
+++ b/solution.py
@@ -175,13 +175,15 @@
                     direct(piece, target.at[layer], {"dp": other})
                 keep(source.at[layer] if kind[0] == "turn" else source, target.at[layer])
             elif kind[0] == "line":
-                absolute, parts = kind[1:]
+                absolute, parts, limit = kind[1:]
                 size = source.shape[0] // parts
-                for part, way in itertools.product(range(parts), (1, -1)):
+                steps = limit or depth - 1
+                ways = (1,) if limit else (1, -1)
+                for part, way in itertools.product(range(parts), ways):
                     behind = layer if way == 1 else depth - 1 - layer
                     onward = layer + way
                     more = (onward >= 0) & (onward < depth)
-                    mine = [next(slots) for _ in range(1, depth)]
+                    mine = [next(slots) for _ in range(steps)]
                     some = pl.ds(part * size, size)
 
                     def held(step, where, way=way, some=some):
@@ -198,11 +200,11 @@
                         )
 
                     begin.append((more, sending(1)))
-                    for step in range(1, depth):
+                    for step in range(1, steps + 1):
                         sent.append((more & (behind >= step - 1), sending(step)))
                         block = held(step, layer)
                         arrival = remote(block, block, {"dp": onward}, mine[step - 1])
-                        nexts = [(more, sending(step + 1))] if step + 1 < depth else []
+                        nexts = [(more, sending(step + 1))] if step < steps else []
                         when = 4 * step + part
                         follow.append((when, step - 1, behind >= step, arrival, nexts))
                 if absolute:
@@ -273,10 +275,10 @@
             shape = (len(distances),) + (shape[1:] if split else shape)
             copies += len(distances)
         elif name == "line":
-            parts = item[3] if len(item) > 3 else 1
-            kinds.append((name, item[2], parts))
-            shape = (depth if item[2] else depth - 1,) + shape
-            copies += 2 * (depth - 1) * parts
+            parts, limit = (item[3:] + (1, 0)[len(item) - 3 :])[:2]
+            kinds.append((name, item[2], parts, limit))
+            shape = (depth if item[2] else limit or depth - 1,) + shape
+            copies += (limit or 2 * (depth - 1)) * parts
         else:
             kinds.append((name,))
             if name in ("share", "collect"):
@@ -307,7 +309,7 @@
         self.scratch = list(scratch)
 
 
-def exchange(sizes, name, number, *items, before=None, after=None, cover=None, landing=(), shared=()):
+def exchange(sizes, name, number, *items, before=None, after=None, cover=None, landing=(), shared=(), delayed=()):
     kinds, moved, sems = planned(sizes, items)
     stages = [stage for stage in (before, after) if stage]
     operands = []
@@ -338,6 +340,7 @@
     shared_at = take(list(shared))
     needed = sorted({o.index for o in (after.operands if after else ()) if isinstance(o, Got)})
     others = [i for i in range(len(items)) if i not in needed]
+    prompt = [i for i in range(len(items)) if i not in delayed]
     later = range(1, 2 * sizes[2])
     cover_at = take(cover.scratch) if cover else slice(0, 0)
     copies = len(operands) + len(outs) + len(late)
@@ -371,7 +374,7 @@
         if cover:
             cover.begin(work_refs, refs[cover_at])
         moves.barrier()
-        moves.start()
+        moves.start(prompt)
         if before:
             for load in loads[:split]:
                 load.wait()
@@ -380,10 +383,13 @@
                 store.start()
         if cover:
             cover.run(work_refs, made_refs, refs[cover_at])
-        moves.relay(None, (0,))
+        moves.relay(prompt, (0,))
+        moves.start(delayed)
         if after:
             moves.relay(needed, later)
             moves.finish(needed)
+        moves.relay(delayed, (0,))
+        if after:
             for load in late_loads:
                 load.start()
             for load in loads[split:]:
@@ -540,8 +546,10 @@
         own[:, i * LANES : (i + 1) * LANES] = blocks[i, own_rows(own.shape[0]), :]
 
 
-def doubled(pair, keys_ref, values_ref, at):
+def doubled(pair, keys_ref, values_ref, at, distance=0):
     wide = pair.astype(jnp.float32)
+    if distance:
+        wide = jnp.where(lax.axis_index("dp") >= distance, wide, 0.0)
     other = pltpu.roll(wide, LANES // 2, 1)
     keys = lanes_of(wide.shape) < LANES // 2
     keys_ref[at] = jnp.where(keys, wide, other).astype(jnp.bfloat16)
@@ -615,7 +623,7 @@
 def attend_rest_body(far, start, mixed, log_total, keys, values, queries, out, tops, totals):
     last, tokens = far.shape[0], far.shape[1]
     for d in range(1, last + 1):
-        doubled(far[d - 1], keys, values, last - d)
+        doubled(far[d - 1], keys, values, last - d, d)
 
     def tile(rows, row, step):
         starts = start[pl.ds(pl.multiple_of(row, step), step), :]
@@ -649,7 +657,7 @@
     last = far.shape[0]
     doubled(pair[...], keys, values, last)
     for d in range(1, last + 1):
-        doubled(far[d - 1], keys, values, last - d)
+        doubled(far[d - 1], keys, values, last - d, d)
     queries[...] = per_head(query[...].astype(jnp.float32)).astype(jnp.bfloat16)
 
     def tile(rows, row, step):
@@ -769,7 +777,7 @@
     attn_grad[...] = (RESIDUAL_SCALE * total).astype(jnp.bfloat16)
 
 
-def project_back_body(query_grad, pair_grad, returned, normed, w_query, w_pair, cosine, sine, output_turned, logit, rows, gains, gain_moe, partial, sums, output_first, output_last, gain_parts):
+def project_back_body(query_grad, pair_grad, returned, normed, w_query, w_pair, cosine, sine, output_turned, logit, rows, gains, gain_moe, partial, sums, output_first, output_last, gain_parts, pairs):
     layer = lax.axis_index("dp")
     depth = lax.axis_size("dp")
     total = pair_grad[...]
@@ -781,9 +789,18 @@
     turned = total * cosine[...] - flipped(total) * sine[...]
     pair_low = jnp.where(keys, turned, total).astype(jnp.bfloat16)
     query_low = query_grad[...]
-    whole = dot(query_low, w_query[...], 1, 1) + dot(pair_low, w_pair[...], 1, 1)
-    partial[...] = whole.astype(jnp.bfloat16)
-    gain_attn = jnp.sum(whole * normed[...].astype(jnp.float32), axis=0, keepdims=True)
+    pairs[...] = pair_low
+    step = 256
+
+    def piece(i, gain_sum):
+        at = pl.ds(pl.multiple_of(i * step, step), step)
+        whole = dot(query_grad[at, :], w_query[...], 1, 1) + dot(pairs[at, :], w_pair[...], 1, 1)
+        partial[at, :] = whole.astype(jnp.bfloat16)
+        named = whole * normed[at, :].astype(jnp.float32)
+        return gain_sum + jnp.sum(named, axis=0, keepdims=True)
+
+    gain_attn = jnp.zeros((1, normed.shape[1]), jnp.float32)
+    gain_attn = lax.fori_loop(0, normed.shape[0] // step, piece, gain_attn)
     gain_attn = gain_attn / gain_row(gains)
     gain_parts[...] = jnp.zeros_like(gain_parts)
     for i in range(gain_parts.shape[0]):
@@ -1103,7 +1120,8 @@
     sums, smalls = refs[: 2 * pieces], refs[2 * pieces : 2 * pieces + 6]
     gin, gout, *others = refs[2 * pieces + 6 : 2 * pieces + 16]
     block_out, in_grad, gain_attn, gain_moe, query, pair, output, router = others
-    in_low, out_low, in_full, out_full, load_sem, store_sem = refs[2 * pieces + 16 :]
+    in_low, out_low, in_full, out_full, *refs = refs[2 * pieces + 16 :]
+    held, (load_sem, store_sem, small_sem) = refs[:6], refs[6:]
     ring = in_full.shape[0]
 
     def load(k, i):
@@ -1112,13 +1130,22 @@
         return pltpu.make_async_copy(source, low.at[i], load_sem.at[k, i])
 
     def store(k, i):
-        held, target = ((in_full, gin), (out_full, gout))[k]
-        return pltpu.make_async_copy(held.at[i % ring], target.at[i], store_sem.at[k, i % ring])
+        made, target = ((in_full, gin), (out_full, gout))[k]
+        return pltpu.make_async_copy(made.at[i % ring], target.at[i], store_sem.at[k, i % ring])
 
     for i in range(total):
         for k in range(2):
             load(k, i).start()
-    blocks, in_blocks, gains, summed, output_first, output_last = smalls
+        if i == 0:
+            fetched = [
+                pltpu.make_async_copy(a, b, small_sem.at[j])
+                for j, (a, b) in enumerate(zip(smalls, held))
+            ]
+            for copy in fetched:
+                copy.start()
+    for copy in fetched:
+        copy.wait()
+    blocks, in_blocks, gains, summed, output_first, output_last = held
     width = gout.shape[2]
     for i in range(blocks.shape[0]):
         at = pl.ds(i * blocks.shape[1], blocks.shape[1])
@@ -1145,8 +1172,8 @@
             load(k, i).wait()
             if i >= ring:
                 store(k, i - ring).wait()
-        for low, held in ((in_low, in_full), (out_low, out_full)):
-            widened(low.at[i], held.at[i % ring])
+        for low, made in ((in_low, in_full), (out_low, out_full)):
+            widened(low.at[i], made.at[i % ring])
         for k in range(2):
             store(k, i).start()
     for i in range(total - ring, total):
@@ -1176,12 +1203,13 @@
     ring = min(4, total)
     gin, *others = pl.pallas_call(
         functools.partial(outputs_body, count, total),
-        in_specs=[HBM] * (2 * len(in_sums)) + [FULL] * len(smalls),
+        in_specs=[HBM] * (2 * len(in_sums) + len(smalls)),
         out_specs=(HBM, HBM) + (FULL,) * (len(shapes) - 2),
         out_shape=tuple(jax.ShapeDtypeStruct(*shape) for shape in shapes),
         scratch_shapes=[pltpu.VMEM((total,) + s, low) for s in large]
         + [pltpu.VMEM((ring,) + s, full) for s in large]
-        + [pltpu.SemaphoreType.DMA((2, total)), pltpu.SemaphoreType.DMA((2, ring))],
+        + [pltpu.VMEM(a.shape, a.dtype) for a in smalls]
+        + [pltpu.SemaphoreType.DMA(s) for s in ((2, total), (2, ring), (len(smalls),))],
         name="outputs",
     )(*in_sums, *out_sums, *smalls)
     gin = gin.reshape(total, width, parts, 2, LANES).transpose(0, 1, 3, 2, 4)
@@ -1243,6 +1271,7 @@
             Made(1),
         ),
         landing=(0,),
+        delayed=(6,),
     )
 
     stack = (hop_count + 1,) + block
@@ -1253,7 +1282,7 @@
         sizes,
         "shift_pairs",
         1,
-        ("shift", pair, hops, False),
+        ("line", pair, False, 2, hop_count),
         ("gather", w_output, False, 4),
         before=Stage(
             attend_first_body,
@@ -1310,7 +1339,7 @@
         "gather_rows",
         3,
         ("gather", rows_own, False, 2),
-        ("line", rows_own, False, 2),
+        ("line", rows_own, False, 4),
     )
     rows_near = rows_blocks.reshape(tok_rows, -1)
     parts = hidden // LANES
@@ -1432,6 +1461,7 @@
             rows_near,
             gains,
             gain_moe_part,
+            scratch=[pltpu.VMEM(block, low)],
         ),
         landing=(0, 2),
     )

time: 214 us -> 216 us (level); the launches traced: 214 us -> 212 us
  no operation moved by 1% of the time
where the time goes in v1:
time: 216 us; the launch traced here: 212 us
  Pallas kernels  211 us (98%)
    pallas_call x9, Pallas kernels, exchange(): pl.pallas_call(body, out_shape=tuple((shape(s) for s in outs + made_shape...  160 us
    pallas_call x1, Pallas kernels, local_experts(): pl.pallas_call(functools.partial(local_experts_body, sizes, kinds), grid=...  36.6 us
    pallas_call x1, Pallas kernels, outputs(): pl.pallas_call(functools.partial(outputs_body, count, total), in_specs=[H...  14.9 us

profile of v1, /device:TPU:0, one launch (start us, length us, event | category | flops | bytes accessed | tf_op | source)
XLA Modules:
  0.0 212.2 jit_solution(2541217442329405451)
XLA Ops:
  0.6 21.7 %gather_tokens.1 = (f32[512,128]{1,0:T(8,128)}, f32[512,128]{1,0:T(8,128)}, bf16[512,1024]{1,0:T(8,128)(2,1)}, bf16[512,128]{1,0:T(8,128)(2,1)}, bf16[512,128]{1...) custom-call(bf16[1024,128]{1,0:T(8,128)(2,1)} %refs_3_.1, ...), custom_call_target="tpu_custom_call" | custom-call | tf_op jit(solution)/shard_map/gather_tokens/pallas_call | solution.py:421
  22.3 16.3 %shift_pairs.1 = (bf16[64,1024]{1,0:T(8,128)(2,1)}, bf16[8,128,512]{2,1,0:T(8,128)(2,1)}, bf16[3,128,512]{2,1,0:T(8,128)(2,1)}, s32[512,1]{1,0:T(8,128)}, bf16[5...) custom-call(bf16[8,512,128]{2,1,0:T(8,128)(2,1)} %get-tuple-element.85.ref, ...), custom_call_target="tpu_custom_call" | custom-call | tf_op jit(solution)/shard_map/shift_pairs/pallas_call | solution.py:421
  38.6 7.9 %swap_mixed.1 = (bf16[64,1152]{1,0:T(8,128)(2,1)}, f32[64,1024]{1,0:T(8,128)}, f32[64,128]{1,0:T(8,128)}) custom-call(bf16[64,1024]{1,0:T(8,128)(2,1)} %get-tuple-element.91.refs_0_.refs_1_, bf16[1024,1024]{1,0:T(8,128)(2,1)} %bitcast.45, bf16[8,1,128]{2,1,0:T(2,128)(2,1)} %get-tuple-element.93.refs_2_.refs_3_, ...), custom_call_target="tpu_custom_call" | custom-call | tf_op jit(solution)/shard_map/swap_mixed/pallas_call | solution.py:421
  46.4 15.7 %gather_rows.1 = (bf16[8,64,1152]{2,1,0:T(8,128)(2,1)}, bf16[3,64,1152]{2,1,0:T(8,128)(2,1)}) custom-call(bf16[64,1152]{1,0:T(8,128)(2,1)} %get-tuple-element.98.refs_0_.refs_1_, bf16[64,1152]{1,0:T(8,128)(2,1)} %get-tuple-element.98.refs_0_.refs_1_), custom_call_target="tpu_custom_call" | custom-call | tf_op jit(solution)/shard_map/gather_rows/pallas_call | solution.py:421
  62.1 36.6 %local_experts.1 = (bf16[512,1024]{1,0:T(8,128)(2,1)}, bf16[512,1152]{1,0:T(8,128)(2,1)}, bf16[8,1024,512]{2,1,0:T(8,128)(2,1)}, bf16[8,512,1024]{2,1,0:T(8,128)...) custom-call(bf16[512,1152]{1,0:T(8,128)(2,1)} %bitcast.43, ...), custom_call_target="tpu_custom_call" | custom-call | tf_op jit(solution)/shard_map/local_experts/pallas_call | solution.py:937
  98.7 17.9 %swap_back.1 = (f32[64,1024]{1,0:T(8,128)}, bf16[64,1024]{1,0:T(8,128)(2,1)}, bf16[64,128]{1,0:T(8,128)(2,1)}, f32[1,1024]{1,0:T(1,128)}, bf16[2,4096,128]{2,1,0:T(8,128)(2,1)}, /*index=5*/bf16[2,256,1024]{2,1,0:T(8,128)(2,1)}) custom-call(bf16[64,1024]{1,0:T(8,128)(2,1)} %get-tuple-element.90.refs_0_, f32[64,1024]{1,0:T(8,128)} %get-tuple-element.96.refs_1_.refs_2_, ...), custom_call_target="tpu_custom_call" | custom-call | tf_op jit(solution)/shard_map/swap_back/pallas_call | solution.py:421
  116.7 20.3 %gather_attn_grad.1 = (bf16[512,128]{1,0:T(8,128)(2,1)}, f32[512,128]{1,0:T(8,128)}, bf16[2,512,128]{2,1,0:T(8,128)(2,1)}, bf16[8,128,128]{2,1,0:T(8,128)(2,1)}, bf16[8,64,128]{2,1,0:T(8,128)(2,1)}) custom-call(bf16[512,128]{1,0:T(8,128)(2,1)} %get-tuple-element.87.refs_2_.refs_0_, bf16[512,128]{1,0:T(8,128)(2,1)} %get-tuple-element.88.refs_3_.refs_6_.refs_1_, ...), custom_call_target="tpu_custom_call" | custom-call | tf_op jit(solution)/shard_map/gather_attn_grad/pallas_call | solution.py:421
  136.9 20.6 %shift_grads.1 = (bf16[512,1024]{1,0:T(8,128)(2,1)}, bf16[2176,128]{1,0:T(8,128)(2,1)}, bf16[128,128]{1,0:T(8,128)(2,1)}, bf16[128,128]{1,0:T(8,128)(2,1)}, f32[...) custom-call(bf16[512,128]{1,0:T(8,128)(2,1)} %get-tuple-element.117., ...), custom_call_target="tpu_custom_call" | custom-call | tf_op jit(solution)/shard_map/shift_grads/pallas_call | solution.py:421
  157.6 19.0 %swap_partial.1 = (bf16[8,64,128]{2,1,0:T(8,128)(2,1)}, bf16[8,64,128]{2,1,0:T(8,128)(2,1)}, f32[8,128]{1,0:T(8,128)}, bf16[544,128]{1,0:T(8,128)(2,1)}, bf16[2,...) custom-call(bf16[8,64,1024]{2,1,0:T(8,128)(2,1)} %get-tuple-element.127.refs_0_, ...), custom_call_target="tpu_custom_call" | custom-call | tf_op jit(solution)/shard_map/swap_partial/pallas_call | solution.py:421
  176.6 20.2 %swap_results.1 = (bf16[2,4096,128]{2,1,0:T(8,128)(2,1)}, bf16[2,256,1024]{2,1,0:T(8,128)(2,1)}, bf16[8,64,128]{2,1,0:T(8,128)(2,1)}, bf16[8,64,128]{2,1,0:T(8,1...) custom-call(bf16[8,1024,512]{2,1,0:T(8,128)(2,1)} %get-tuple-element.103.refs_5_.refs_11_, ...), custom_call_target="tpu_custom_call" | custom-call | tf_op jit(solution)/shard_map/swap_results/pallas_call | solution.py:421
  196.8 14.9 %outputs.1 = (f32[8,4096,128]{2,1,0:T(8,128)}, f32[8,256,1024]{2,1,0:T(8,128)}, bf16[512,128]{1,0:T(8,128)(2,1)}, bf16[512,128]{1,0:T(8,128)(2,1)}, f32[1,128]{1...) custom-call(bf16[2,4096,128]{2,1,0:T(8,128)(2,1)} %get-tuple-element, ...), custom_call_target="tpu_custom_call" | custom-call | tf_op jit(solution)/shard_map/outputs/pallas_call | solution.py:1204

commit v2 on v1

--- a/solution.py
+++ b/solution.py
@@ -481,9 +481,10 @@
 
 
 def added(blocks):
-    return functools.reduce(
-        jnp.add, [blocks[i].astype(jnp.float32) for i in range(blocks.shape[0])]
-    )
+    def more(i, total):
+        return total + blocks[i].astype(jnp.float32)
+
+    return lax.fori_loop(1, blocks.shape[0], more, blocks[0].astype(jnp.float32))
 
 
 def own_rows(count):
@@ -777,7 +778,7 @@
     attn_grad[...] = (RESIDUAL_SCALE * total).astype(jnp.bfloat16)
 
 
-def project_back_body(query_grad, pair_grad, returned, normed, w_query, w_pair, cosine, sine, output_turned, logit, rows, gains, gain_moe, partial, sums, output_first, output_last, gain_parts, pairs):
+def project_back_body(query_grad, pair_grad, returned, normed, w_query, w_pair, cosine, sine, output_turned, logit, rows, gains, gain_moe, partial, sums, output_first, output_last, gain_parts):
     layer = lax.axis_index("dp")
     depth = lax.axis_size("dp")
     total = pair_grad[...]
@@ -789,18 +790,9 @@
     turned = total * cosine[...] - flipped(total) * sine[...]
     pair_low = jnp.where(keys, turned, total).astype(jnp.bfloat16)
     query_low = query_grad[...]
-    pairs[...] = pair_low
-    step = 256
-
-    def piece(i, gain_sum):
-        at = pl.ds(pl.multiple_of(i * step, step), step)
-        whole = dot(query_grad[at, :], w_query[...], 1, 1) + dot(pairs[at, :], w_pair[...], 1, 1)
-        partial[at, :] = whole.astype(jnp.bfloat16)
-        named = whole * normed[at, :].astype(jnp.float32)
-        return gain_sum + jnp.sum(named, axis=0, keepdims=True)
-
-    gain_attn = jnp.zeros((1, normed.shape[1]), jnp.float32)
-    gain_attn = lax.fori_loop(0, normed.shape[0] // step, piece, gain_attn)
+    whole = dot(query_low, w_query[...], 1, 1) + dot(pair_low, w_pair[...], 1, 1)
+    partial[...] = whole.astype(jnp.bfloat16)
+    gain_attn = jnp.sum(whole * normed[...].astype(jnp.float32), axis=0, keepdims=True)
     gain_attn = gain_attn / gain_row(gains)
     gain_parts[...] = jnp.zeros_like(gain_parts)
     for i in range(gain_parts.shape[0]):
@@ -822,11 +814,8 @@
     gain_sum[...] = added(gain_blocks)
     summed[...] = added(turned).astype(jnp.bfloat16)
     width = own.shape[1]
-    normed_grad = blocks[0].astype(jnp.float32)
-    branch = moe[0].astype(jnp.float32)
-    for i in range(1, blocks.shape[0]):
-        normed_grad = normed_grad + blocks[i].astype(jnp.float32)
-        branch = branch + moe[i].astype(jnp.float32)
+    normed_grad = added(blocks)
+    branch = added(moe)
     value = own[...].astype(jnp.float32)
     scale = lax.rsqrt(jnp.mean(value * value, axis=1, keepdims=True) + EPSILON)
     scaled = normed_grad * gain_row(gains)
@@ -906,10 +895,10 @@
 
     @pl.when(step == steps - 1)
     def _():
+        moves.relay([1], (1,))
         widened(moe_acc, moe_ref)
         widened(back_acc, back_ref.at[:, :width])
         back_ref[:, width:] = share[...].T.astype(jnp.bfloat16)
-        moves.relay([1], (1,))
         moves.finish()
 
 
@@ -1143,30 +1132,32 @@
             ]
             for copy in fetched:
                 copy.start()
-    for copy in fetched:
-        copy.wait()
-    blocks, in_blocks, gains, summed, output_first, output_last = held
-    width = gout.shape[2]
-    for i in range(blocks.shape[0]):
-        at = pl.ds(i * blocks.shape[1], blocks.shape[1])
-        block_out[at, :] = blocks[i]
-        in_grad[at, :] = in_blocks[i]
-    gain_sum = jnp.sum(gains[...], axis=0)
-    gain_attn[...] = gain_sum[0:1, :]
-    gain_moe[...] = gain_sum[1:2, :]
-    query[...] = summed[:width, :].astype(jnp.float32)
-    pair[...] = summed[width : 2 * width, :].astype(jnp.float32)
-    router[...] = summed[2 * width : 2 * width + router.shape[0], :].astype(jnp.float32)
-    half = output_first.shape[1]
-    for i in range(width // half):
-        from_first = i % 2 == 0
-        rows = (output_first if from_first else output_last)[i // 2].astype(jnp.float32)
-        for j in range(max(1, half // LANES)):
-            place = i * half + j * LANES
-            at = place // LANES
-            part = rows[j * LANES : (j + 1) * LANES, :]
-            first = place % LANES
-            output[first : first + part.shape[0], at * LANES : (at + 1) * LANES] = part
+    def small():
+        for copy in fetched:
+            copy.wait()
+        blocks, in_blocks, gains, summed, output_first, output_last = held
+        width = gout.shape[2]
+        for i in range(blocks.shape[0]):
+            at = pl.ds(i * blocks.shape[1], blocks.shape[1])
+            block_out[at, :] = blocks[i]
+            in_grad[at, :] = in_blocks[i]
+        gain_sum = jnp.sum(gains[...], axis=0)
+        gain_attn[...] = gain_sum[0:1, :]
+        gain_moe[...] = gain_sum[1:2, :]
+        query[...] = summed[:width, :].astype(jnp.float32)
+        pair[...] = summed[width : 2 * width, :].astype(jnp.float32)
+        router[...] = summed[2 * width : 2 * width + router.shape[0], :].astype(jnp.float32)
+        half = output_first.shape[1]
+        for i in range(width // half):
+            from_first = i % 2 == 0
+            rows = (output_first if from_first else output_last)[i // 2].astype(jnp.float32)
+            for j in range(max(1, half // LANES)):
+                place = i * half + j * LANES
+                at = place // LANES
+                part = rows[j * LANES : (j + 1) * LANES, :]
+                first = place % LANES
+                output[first : first + part.shape[0], at * LANES : (at + 1) * LANES] = part
+
     for i in range(total):
         for k in range(2):
             load(k, i).wait()
@@ -1176,6 +1167,8 @@
             widened(low.at[i], made.at[i % ring])
         for k in range(2):
             store(k, i).start()
+        if i == 1:
+            small()
     for i in range(total - ring, total):
         for k in range(2):
             store(k, i).wait()
@@ -1461,7 +1454,6 @@
             rows_near,
             gains,
             gain_moe_part,
-            scratch=[pltpu.VMEM(block, low)],
         ),
         landing=(0, 2),
     )

time: 216 us -> 212 us (0.981); the launches traced: 212 us -> 212 us
  no operation moved by 1% of the time
where the time goes in v2:
time: 212 us
  Pallas kernels  211 us (100%)
    pallas_call x9, Pallas kernels, exchange(): pl.pallas_call(body, out_shape=tuple((shape(s) for s in outs + made_shape...  159 us
    pallas_call x1, Pallas kernels, local_experts(): pl.pallas_call(functools.partial(local_experts_body, sizes, kinds), grid=...  36.6 us
    pallas_call x1, Pallas kernels, outputs(): pl.pallas_call(functools.partial(outputs_body, count, total), in_specs=[H...  15.3 us

profile of v2, /device:TPU:0, one launch (start us, length us, event | category | flops | bytes accessed | tf_op | source)
XLA Modules:
  0.0 211.7 jit_solution(14347127766138214248)
XLA Ops:
  0.6 21.7 %gather_tokens.1 = (f32[512,128]{1,0:T(8,128)}, f32[512,128]{1,0:T(8,128)}, bf16[512,1024]{1,0:T(8,128)(2,1)}, bf16[512,128]{1,0:T(8,128)(2,1)}, bf16[512,128]{1...) custom-call(bf16[1024,128]{1,0:T(8,128)(2,1)} %refs_3_.1, ...), custom_call_target="tpu_custom_call" | custom-call | tf_op jit(solution)/shard_map/gather_tokens/pallas_call | solution.py:421
  22.3 16.3 %shift_pairs.1 = (bf16[64,1024]{1,0:T(8,128)(2,1)}, bf16[8,128,512]{2,1,0:T(8,128)(2,1)}, bf16[3,128,512]{2,1,0:T(8,128)(2,1)}, s32[512,1]{1,0:T(8,128)}, bf16[5...) custom-call(bf16[8,512,128]{2,1,0:T(8,128)(2,1)} %get-tuple-element.85.ref, ...), custom_call_target="tpu_custom_call" | custom-call | tf_op jit(solution)/shard_map/shift_pairs/pallas_call | solution.py:421
  38.6 7.9 %swap_mixed.1 = (bf16[64,1152]{1,0:T(8,128)(2,1)}, f32[64,1024]{1,0:T(8,128)}, f32[64,128]{1,0:T(8,128)}) custom-call(bf16[64,1024]{1,0:T(8,128)(2,1)} %get-tuple-element.91.refs_0_.refs_1_, bf16[1024,1024]{1,0:T(8,128)(2,1)} %bitcast.45, bf16[8,1,128]{2,1,0:T(2,128)(2,1)} %get-tuple-element.93.refs_2_.refs_3_, ...), custom_call_target="tpu_custom_call" | custom-call | tf_op jit(solution)/shard_map/swap_mixed/pallas_call | solution.py:421
  46.4 15.7 %gather_rows.1 = (bf16[8,64,1152]{2,1,0:T(8,128)(2,1)}, bf16[3,64,1152]{2,1,0:T(8,128)(2,1)}) custom-call(bf16[64,1152]{1,0:T(8,128)(2,1)} %get-tuple-element.98.refs_0_.refs_1_, bf16[64,1152]{1,0:T(8,128)(2,1)} %get-tuple-element.98.refs_0_.refs_1_), custom_call_target="tpu_custom_call" | custom-call | tf_op jit(solution)/shard_map/gather_rows/pallas_call | solution.py:421
  62.1 36.6 %local_experts.1 = (bf16[512,1024]{1,0:T(8,128)(2,1)}, bf16[512,1152]{1,0:T(8,128)(2,1)}, bf16[8,1024,512]{2,1,0:T(8,128)(2,1)}, bf16[8,512,1024]{2,1,0:T(8,128)...) custom-call(bf16[512,1152]{1,0:T(8,128)(2,1)} %bitcast.43, ...), custom_call_target="tpu_custom_call" | custom-call | tf_op jit(solution)/shard_map/local_experts/pallas_call | solution.py:926
  98.7 17.9 %swap_back.1 = (f32[64,1024]{1,0:T(8,128)}, bf16[64,1024]{1,0:T(8,128)(2,1)}, bf16[64,128]{1,0:T(8,128)(2,1)}, f32[1,1024]{1,0:T(1,128)}, bf16[2,4096,128]{2,1,0:T(8,128)(2,1)}, /*index=5*/bf16[2,256,1024]{2,1,0:T(8,128)(2,1)}) custom-call(bf16[64,1024]{1,0:T(8,128)(2,1)} %get-tuple-element.90.refs_0_, f32[64,1024]{1,0:T(8,128)} %get-tuple-element.96.refs_1_.refs_2_, ...), custom_call_target="tpu_custom_call" | custom-call | tf_op jit(solution)/shard_map/swap_back/pallas_call | solution.py:421
  116.7 19.9 %gather_attn_grad.1 = (bf16[512,128]{1,0:T(8,128)(2,1)}, f32[512,128]{1,0:T(8,128)}, bf16[2,512,128]{2,1,0:T(8,128)(2,1)}, bf16[8,128,128]{2,1,0:T(8,128)(2,1)}, bf16[8,64,128]{2,1,0:T(8,128)(2,1)}) custom-call(bf16[512,128]{1,0:T(8,128)(2,1)} %get-tuple-element.87.refs_2_.refs_0_, bf16[512,128]{1,0:T(8,128)(2,1)} %get-tuple-element.88.refs_3_.refs_6_.refs_1_, ...), custom_call_target="tpu_custom_call" | custom-call | tf_op jit(solution)/shard_map/gather_attn_grad/pallas_call | solution.py:421
  136.6 20.5 %shift_grads.1 = (bf16[512,1024]{1,0:T(8,128)(2,1)}, bf16[2176,128]{1,0:T(8,128)(2,1)}, bf16[128,128]{1,0:T(8,128)(2,1)}, bf16[128,128]{1,0:T(8,128)(2,1)}, f32[...) custom-call(bf16[512,128]{1,0:T(8,128)(2,1)} %get-tuple-element.117., ...), custom_call_target="tpu_custom_call" | custom-call | tf_op jit(solution)/shard_map/shift_grads/pallas_call | solution.py:421
  157.1 19.3 %swap_partial.1 = (bf16[8,64,128]{2,1,0:T(8,128)(2,1)}, bf16[8,64,128]{2,1,0:T(8,128)(2,1)}, f32[8,128]{1,0:T(8,128)}, bf16[544,128]{1,0:T(8,128)(2,1)}, bf16[2,...) custom-call(bf16[8,64,1024]{2,1,0:T(8,128)(2,1)} %get-tuple-element.127.refs_0_, ...), custom_call_target="tpu_custom_call" | custom-call | tf_op jit(solution)/shard_map/swap_partial/pallas_call | solution.py:421
  176.4 19.8 %swap_results.1 = (bf16[2,4096,128]{2,1,0:T(8,128)(2,1)}, bf16[2,256,1024]{2,1,0:T(8,128)(2,1)}, bf16[8,64,128]{2,1,0:T(8,128)(2,1)}, bf16[8,64,128]{2,1,0:T(8,1...) custom-call(bf16[8,1024,512]{2,1,0:T(8,128)(2,1)} %get-tuple-element.103.refs_5_.refs_11_, ...), custom_call_target="tpu_custom_call" | custom-call | tf_op jit(solution)/shard_map/swap_results/pallas_call | solution.py:421
  196.3 15.3 %outputs.1 = (f32[8,4096,128]{2,1,0:T(8,128)}, f32[8,256,1024]{2,1,0:T(8,128)}, bf16[512,128]{1,0:T(8,128)(2,1)}, bf16[512,128]{1,0:T(8,128)(2,1)}, f32[1,128]{1...) custom-call(bf16[2,4096,128]{2,1,0:T(8,128)(2,1)} %get-tuple-element, ...), custom_call_target="tpu_custom_call" | custom-call | tf_op jit(solution)/shard_map/outputs/pallas_call | solution.py:1197

commit v3 on v2

--- a/solution.py
+++ b/solution.py
@@ -718,9 +718,19 @@
 
 
 def router_rows(router):
-    rows = beside(router).astype(jnp.float32)
-    blank = jnp.zeros((LANES - rows.shape[0], rows.shape[1]), jnp.float32)
+    rows = beside(router)
+    blank = jnp.zeros((LANES - rows.shape[0], rows.shape[1]), rows.dtype)
     return jnp.concatenate([rows, blank], axis=0)
+
+
+def full_dot(wide, low, left=1, right=0):
+    parts, rest = [], wide
+    for _ in range(3):
+        parts.append(rest.astype(jnp.bfloat16))
+        rest = rest - parts[-1].astype(jnp.float32)
+    count = wide.shape[0]
+    sums = dot(jnp.concatenate(parts, axis=0), low, left, right)
+    return sums[:count] + (sums[count : 2 * count] + sums[2 * count :])
 
 
 def middle_body(mixed, own, w_output, gains, router, ids_turned, rows, middle, weights, ids_ref):
@@ -731,7 +741,7 @@
     middle[...] = value
     scale = lax.rsqrt(jnp.mean(value * value, axis=1, keepdims=True) + EPSILON)
     normed = value * scale * gain_row(gains)
-    logits = dot(normed, router_rows(router), 1, 1, precision=HIGH)
+    logits = full_dot(normed, router_rows(router), 1, 1)
     count = own.shape[0]
     ids_ref[...] = ids_turned[...].astype(jnp.float32).T
     ids = ids_ref[own_rows(count), :]
@@ -764,7 +774,7 @@
     mean = jnp.sum(share * weight_grad, axis=1, keepdims=True)
     logit = share * (weight_grad - mean)
     logit_grad[...] = logit.astype(jnp.bfloat16)
-    normed_grad = normed_grad + dot(logit, router_rows(router), precision=HIGH)
+    normed_grad = normed_grad + full_dot(logit, router_rows(router))
     scale = lax.rsqrt(jnp.mean(value * value, axis=1, keepdims=True) + EPSILON)
     gain_part[...] = jnp.sum(normed_grad * value * scale, axis=0, keepdims=True)
     scaled = normed_grad * gain_row(gains)
@@ -1167,7 +1177,7 @@
             widened(low.at[i], made.at[i % ring])
         for k in range(2):
             store(k, i).start()
-        if i == 1:
+        if i == total - 3:
             small()
     for i in range(total - ring, total):
         for k in range(2):
@@ -1396,6 +1406,7 @@
         5,
         ("gather", attn_grad, False, 2),
         ("gather", logit_grad),
+        delayed=(1,),
         before=Stage(attend_again_body, [], query, pair, far, start, log_total),
         after=Stage(
             attend_back_body,

time: 212 us -> 210 us (level)
  no operation moved by 1% of the time
where the time goes in v3:
time: 210 us
  Pallas kernels  209 us (100%)
    pallas_call x9, Pallas kernels, exchange(): pl.pallas_call(body, out_shape=tuple((shape(s) for s in outs + made_shape...  157 us
    pallas_call x1, Pallas kernels, local_experts(): pl.pallas_call(functools.partial(local_experts_body, sizes, kinds), grid=...  36.6 us
    pallas_call x1, Pallas kernels, outputs(): pl.pallas_call(functools.partial(outputs_body, count, total), in_specs=[H...  14.6 us

profile of v3, /device:TPU:0, one launch (start us, length us, event | category | flops | bytes accessed | tf_op | source)
XLA Modules:
  0.0 209.5 jit_solution(15410226444406880633)
XLA Ops:
  0.6 21.7 %gather_tokens.1 = (f32[512,128]{1,0:T(8,128)}, f32[512,128]{1,0:T(8,128)}, bf16[512,1024]{1,0:T(8,128)(2,1)}, bf16[512,128]{1,0:T(8,128)(2,1)}, bf16[512,128]{1...) custom-call(bf16[1024,128]{1,0:T(8,128)(2,1)} %refs_3_.1, ...), custom_call_target="tpu_custom_call" | custom-call | tf_op jit(solution)/shard_map/gather_tokens/pallas_call | solution.py:421
  22.3 16.3 %shift_pairs.1 = (bf16[64,1024]{1,0:T(8,128)(2,1)}, bf16[8,128,512]{2,1,0:T(8,128)(2,1)}, bf16[3,128,512]{2,1,0:T(8,128)(2,1)}, s32[512,1]{1,0:T(8,128)}, bf16[5...) custom-call(bf16[8,512,128]{2,1,0:T(8,128)(2,1)} %get-tuple-element.85.ref, ...), custom_call_target="tpu_custom_call" | custom-call | tf_op jit(solution)/shard_map/shift_pairs/pallas_call | solution.py:421
  38.6 7.4 %swap_mixed.1 = (bf16[64,1152]{1,0:T(8,128)(2,1)}, f32[64,1024]{1,0:T(8,128)}, f32[64,128]{1,0:T(8,128)}) custom-call(bf16[64,1024]{1,0:T(8,128)(2,1)} %get-tuple-element.91.refs_0_.refs_1_, bf16[1024,1024]{1,0:T(8,128)(2,1)} %bitcast.45, bf16[8,1,128]{2,1,0:T(2,128)(2,1)} %get-tuple-element.93.refs_2_.refs_3_, ...), custom_call_target="tpu_custom_call" | custom-call | tf_op jit(solution)/shard_map/swap_mixed/pallas_call | solution.py:421
  46.0 15.7 %gather_rows.1 = (bf16[8,64,1152]{2,1,0:T(8,128)(2,1)}, bf16[3,64,1152]{2,1,0:T(8,128)(2,1)}) custom-call(bf16[64,1152]{1,0:T(8,128)(2,1)} %get-tuple-element.98.refs_0_.refs_1_, bf16[64,1152]{1,0:T(8,128)(2,1)} %get-tuple-element.98.refs_0_.refs_1_), custom_call_target="tpu_custom_call" | custom-call | tf_op jit(solution)/shard_map/gather_rows/pallas_call | solution.py:421
  61.7 36.6 %local_experts.1 = (bf16[512,1024]{1,0:T(8,128)(2,1)}, bf16[512,1152]{1,0:T(8,128)(2,1)}, bf16[8,1024,512]{2,1,0:T(8,128)(2,1)}, bf16[8,512,1024]{2,1,0:T(8,128)...) custom-call(bf16[512,1152]{1,0:T(8,128)(2,1)} %bitcast.43, ...), custom_call_target="tpu_custom_call" | custom-call | tf_op jit(solution)/shard_map/local_experts/pallas_call | solution.py:936
  98.3 17.9 %swap_back.1 = (f32[64,1024]{1,0:T(8,128)}, bf16[64,1024]{1,0:T(8,128)(2,1)}, bf16[64,128]{1,0:T(8,128)(2,1)}, f32[1,1024]{1,0:T(1,128)}, bf16[2,4096,128]{2,1,0:T(8,128)(2,1)}, /*index=5*/bf16[2,256,1024]{2,1,0:T(8,128)(2,1)}) custom-call(bf16[64,1024]{1,0:T(8,128)(2,1)} %get-tuple-element.90.refs_0_, f32[64,1024]{1,0:T(8,128)} %get-tuple-element.96.refs_1_.refs_2_, ...), custom_call_target="tpu_custom_call" | custom-call | tf_op jit(solution)/shard_map/swap_back/pallas_call | solution.py:421
  116.1 18.9 %gather_attn_grad.1 = (bf16[512,128]{1,0:T(8,128)(2,1)}, f32[512,128]{1,0:T(8,128)}, bf16[2,512,128]{2,1,0:T(8,128)(2,1)}, bf16[8,128,128]{2,1,0:T(8,128)(2,1)}, bf16[8,64,128]{2,1,0:T(8,128)(2,1)}) custom-call(bf16[512,128]{1,0:T(8,128)(2,1)} %get-tuple-element.87.refs_2_.refs_0_, bf16[512,128]{1,0:T(8,128)(2,1)} %get-tuple-element.88.refs_3_.refs_6_.refs_1_, ...), custom_call_target="tpu_custom_call" | custom-call | tf_op jit(solution)/shard_map/gather_attn_grad/pallas_call | solution.py:421
  135.0 20.5 %shift_grads.1 = (bf16[512,1024]{1,0:T(8,128)(2,1)}, bf16[2176,128]{1,0:T(8,128)(2,1)}, bf16[128,128]{1,0:T(8,128)(2,1)}, bf16[128,128]{1,0:T(8,128)(2,1)}, f32[...) custom-call(bf16[512,128]{1,0:T(8,128)(2,1)} %get-tuple-element.117., ...), custom_call_target="tpu_custom_call" | custom-call | tf_op jit(solution)/shard_map/shift_grads/pallas_call | solution.py:421
  155.5 19.3 %swap_partial.1 = (bf16[8,64,128]{2,1,0:T(8,128)(2,1)}, bf16[8,64,128]{2,1,0:T(8,128)(2,1)}, f32[8,128]{1,0:T(8,128)}, bf16[544,128]{1,0:T(8,128)(2,1)}, bf16[2,...) custom-call(bf16[8,64,1024]{2,1,0:T(8,128)(2,1)} %get-tuple-element.127.refs_0_, ...), custom_call_target="tpu_custom_call" | custom-call | tf_op jit(solution)/shard_map/swap_partial/pallas_call | solution.py:421
  174.9 19.8 %swap_results.1 = (bf16[2,4096,128]{2,1,0:T(8,128)(2,1)}, bf16[2,256,1024]{2,1,0:T(8,128)(2,1)}, bf16[8,64,128]{2,1,0:T(8,128)(2,1)}, bf16[8,64,128]{2,1,0:T(8,1...) custom-call(bf16[8,1024,512]{2,1,0:T(8,128)(2,1)} %get-tuple-element.103.refs_5_.refs_11_, ...), custom_call_target="tpu_custom_call" | custom-call | tf_op jit(solution)/shard_map/swap_results/pallas_call | solution.py:421
  194.7 14.6 %outputs.1 = (f32[8,4096,128]{2,1,0:T(8,128)}, f32[8,256,1024]{2,1,0:T(8,128)}, bf16[512,128]{1,0:T(8,128)(2,1)}, bf16[512,128]{1,0:T(8,128)(2,1)}, f32[1,128]{1...) custom-call(bf16[2,4096,128]{2,1,0:T(8,128)(2,1)} %get-tuple-element, ...), custom_call_target="tpu_custom_call" | custom-call | tf_op jit(solution)/shard_map/outputs/pallas_call | solution.py:1207

commit v4 on v3

--- a/solution.py
+++ b/solution.py
@@ -10,7 +10,6 @@
 from jax.sharding import PartitionSpec as P
 
 LONGEST = 4096
-HIGH = lax.Precision.HIGHEST
 EPSILON = 1e-05
 RESIDUAL_SCALE = 0.22
 SCORE_SCALE = 0.015625
@@ -858,18 +857,24 @@
     return turned[: LANES // 2] + turned[LANES // 2 :]
 
 
-def local_experts_body(sizes, kinds, rows_ref, grads_ref, in_ref, out_ref, sent_grads, sent_rows, moe_ref, back_ref, flat_ref, in_sum, out_sum, got_grads, got_rows, moe_acc, back_acc, share, weights, spread, *sems):
+def local_experts_body(sizes, kinds, rows_hbm, grads_hbm, in_ref, out_ref, sent_grads, sent_rows, flat_ref, in_sum, out_sum, moe_hbm, back_hbm, got_grads, got_rows, rows_ref, grads_ref, moe_ref, back_ref, moe_acc, back_acc, share, weights, spread, copy_sem, *sems):
     step, steps = pl.program_id(0), pl.num_programs(0)
     each, hidden, width = out_ref.shape
     parts = hidden // LANES
     moves = Moves(sizes, kinds, [sent_grads, sent_rows], [got_grads, got_rows], sems)
+    ends = [(rows_hbm, rows_ref), (grads_hbm, grads_ref), (moe_ref, moe_hbm), (back_ref, back_hbm)]
+    copy = lambda i: pltpu.make_async_copy(*ends[i], copy_sem.at[i])
 
     @pl.when(step == 0)
     def _():
+        copy(0).start()
+        copy(1).start()
         moves.barrier()
         moves.start([0])
         cleared(moe_acc)
         cleared(back_acc)
+        copy(0).wait()
+        copy(1).wait()
         share[...] = jnp.zeros_like(share)
         weights[...] = weight_rows(rows_ref[:, width:])
 
@@ -907,9 +912,13 @@
     def _():
         moves.relay([1], (1,))
         widened(moe_acc, moe_ref)
+        copy(2).start()
         widened(back_acc, back_ref.at[:, :width])
         back_ref[:, width:] = share[...].T.astype(jnp.bfloat16)
+        copy(3).start()
         moves.finish()
+        copy(2).wait()
+        copy(3).wait()
 
 
 def local_experts(sizes, number, rows, grads, w_in, w_out, sent_grads, sent_rows):
@@ -924,34 +933,38 @@
             ("gather", sent_rows, True, sent_rows.shape[0]),
         ],
     )
-    whole = lambda s: pl.BlockSpec(s, lambda e: (0,) * len(s))
     some = lambda s: pl.BlockSpec((each,) + s[1:], lambda e: (e,) + (0,) * (len(s) - 1))
     outs = [
-        (tokens, width),
-        (tokens, wide),
         (experts, width, 2 * hidden),
         (experts, 2 * hidden, width),
         (experts, hidden, width),
+        (tokens, width),
+        (tokens, wide),
     ]
     return pl.pallas_call(
         functools.partial(local_experts_body, sizes, kinds),
         grid=(experts // each,),
         in_specs=[
-            whole(rows.shape),
-            whole(grads.shape),
+            HBM,
+            HBM,
             some(w_in.shape),
             some(w_out.shape),
             HBM,
             HBM,
         ],
-        out_specs=(whole(outs[0]), whole(outs[1]), *[some(s) for s in outs[2:]], HBM, HBM),
+        out_specs=(*[some(s) for s in outs[:3]], HBM, HBM, HBM, HBM),
         out_shape=tuple(jax.ShapeDtypeStruct(s, low) for s in outs) + tuple(shapes),
         scratch_shapes=[
+            pltpu.VMEM(rows.shape, low),
+            pltpu.VMEM(grads.shape, low),
+            pltpu.VMEM((tokens, width), low),
+            pltpu.VMEM((tokens, wide), low),
             pltpu.VMEM((tokens, width), jnp.float32),
             pltpu.VMEM((tokens, width), jnp.float32),
             pltpu.VMEM((LANES, tokens), jnp.float32),
             pltpu.VMEM((LANES // 2, tokens), jnp.float32),
             pltpu.VMEM((each,) + w_in.shape[1:], jnp.float32),
+            pltpu.SemaphoreType.DMA((4,)),
         ]
         + sems,
         compiler_params=pltpu.CompilerParams(collective_id=number, has_side_effects=True),
@@ -1348,7 +1361,7 @@
     parts = hidden // LANES
     in_rows = w_expert_in.reshape(expert_local, width, 2, parts, LANES)
     in_rows = in_rows.transpose(0, 1, 3, 2, 4).reshape(expert_local, -1, LANES)
-    moe_partial, back_partial, in_flat, in_part, out_part, grads_far, rows_far = local_experts(
+    in_flat, in_part, out_part, moe_partial, back_partial, grads_far, rows_far = local_experts(
         sizes,
         9,
         rows_near,

time: 210 us -> 208 us (level)
  no operation moved by 1% of the time
where the time goes in v4:
time: 208 us
  Pallas kernels  207 us (100%)
    pallas_call x9, Pallas kernels, exchange(): pl.pallas_call(body, out_shape=tuple((shape(s) for s in outs + made_shape...  157 us
    pallas_call x1, Pallas kernels, local_experts(): pl.pallas_call(functools.partial(local_experts_body, sizes, kinds), grid=...  35.3 us
    pallas_call x1, Pallas kernels, outputs(): pl.pallas_call(functools.partial(outputs_body, count, total), in_specs=[H...  14.6 us

profile of v4, /device:TPU:0, one launch (start us, length us, event | category | flops | bytes accessed | tf_op | source)
XLA Modules:
  0.0 208.2 jit_solution(14103243525730978433)
XLA Ops:
  0.6 21.7 %gather_tokens.1 = (f32[512,128]{1,0:T(8,128)}, f32[512,128]{1,0:T(8,128)}, bf16[512,1024]{1,0:T(8,128)(2,1)}, bf16[512,128]{1,0:T(8,128)(2,1)}, bf16[512,128]{1...) custom-call(bf16[1024,128]{1,0:T(8,128)(2,1)} %refs_3_.1, ...), custom_call_target="tpu_custom_call" | custom-call | tf_op jit(solution)/shard_map/gather_tokens/pallas_call | solution.py:420
  22.3 16.3 %shift_pairs.1 = (bf16[64,1024]{1,0:T(8,128)(2,1)}, bf16[8,128,512]{2,1,0:T(8,128)(2,1)}, bf16[3,128,512]{2,1,0:T(8,128)(2,1)}, s32[512,1]{1,0:T(8,128)}, bf16[5...) custom-call(bf16[8,512,128]{2,1,0:T(8,128)(2,1)} %get-tuple-element.85.ref, ...), custom_call_target="tpu_custom_call" | custom-call | tf_op jit(solution)/shard_map/shift_pairs/pallas_call | solution.py:420
  38.6 7.4 %swap_mixed.1 = (bf16[64,1152]{1,0:T(8,128)(2,1)}, f32[64,1024]{1,0:T(8,128)}, f32[64,128]{1,0:T(8,128)}) custom-call(bf16[64,1024]{1,0:T(8,128)(2,1)} %get-tuple-element.91.refs_0_.refs_1_, bf16[1024,1024]{1,0:T(8,128)(2,1)} %bitcast.45, bf16[8,1,128]{2,1,0:T(2,128)(2,1)} %get-tuple-element.93.refs_2_.refs_3_, ...), custom_call_target="tpu_custom_call" | custom-call | tf_op jit(solution)/shard_map/swap_mixed/pallas_call | solution.py:420
  46.0 15.7 %gather_rows.1 = (bf16[8,64,1152]{2,1,0:T(8,128)(2,1)}, bf16[3,64,1152]{2,1,0:T(8,128)(2,1)}) custom-call(bf16[64,1152]{1,0:T(8,128)(2,1)} %get-tuple-element.98.refs_0_.refs_1_, bf16[64,1152]{1,0:T(8,128)(2,1)} %get-tuple-element.98.refs_0_.refs_1_), custom_call_target="tpu_custom_call" | custom-call | tf_op jit(solution)/shard_map/gather_rows/pallas_call | solution.py:420
  61.7 35.3 %local_experts.1 = (bf16[8,1024,512]{2,1,0:T(8,128)(2,1)}, bf16[8,512,1024]{2,1,0:T(8,128)(2,1)}, bf16[8,256,1024]{2,1,0:T(8,128)(2,1)}, bf16[512,1024]{1,0:T(8,...) custom-call(bf16[512,1152]{1,0:T(8,128)(2,1)} %bitcast.43, ...), custom_call_target="tpu_custom_call" | custom-call | tf_op jit(solution)/shard_map/local_experts/pallas_call | solution.py:944
  97.0 17.9 %swap_back.1 = (f32[64,1024]{1,0:T(8,128)}, bf16[64,1024]{1,0:T(8,128)(2,1)}, bf16[64,128]{1,0:T(8,128)(2,1)}, f32[1,1024]{1,0:T(1,128)}, bf16[2,4096,128]{2,1,0:T(8,128)(2,1)}, /*index=5*/bf16[2,256,1024]{2,1,0:T(8,128)(2,1)}) custom-call(bf16[64,1024]{1,0:T(8,128)(2,1)} %get-tuple-element.90.refs_0_, f32[64,1024]{1,0:T(8,128)} %get-tuple-element.96.refs_1_.refs_2_, ...), custom_call_target="tpu_custom_call" | custom-call | tf_op jit(solution)/shard_map/swap_back/pallas_call | solution.py:420
  114.9 18.8 %gather_attn_grad.1 = (bf16[512,128]{1,0:T(8,128)(2,1)}, f32[512,128]{1,0:T(8,128)}, bf16[2,512,128]{2,1,0:T(8,128)(2,1)}, bf16[8,128,128]{2,1,0:T(8,128)(2,1)}, bf16[8,64,128]{2,1,0:T(8,128)(2,1)}) custom-call(bf16[512,128]{1,0:T(8,128)(2,1)} %get-tuple-element.87.refs_2_.refs_0_, bf16[512,128]{1,0:T(8,128)(2,1)} %get-tuple-element.88.refs_3_.refs_6_.refs_1_, ...), custom_call_target="tpu_custom_call" | custom-call | tf_op jit(solution)/shard_map/gather_attn_grad/pallas_call | solution.py:420
  133.7 20.5 %shift_grads.1 = (bf16[512,1024]{1,0:T(8,128)(2,1)}, bf16[2176,128]{1,0:T(8,128)(2,1)}, bf16[128,128]{1,0:T(8,128)(2,1)}, bf16[128,128]{1,0:T(8,128)(2,1)}, f32[...) custom-call(bf16[512,128]{1,0:T(8,128)(2,1)} %get-tuple-element.117., ...), custom_call_target="tpu_custom_call" | custom-call | tf_op jit(solution)/shard_map/shift_grads/pallas_call | solution.py:420
  154.1 19.3 %swap_partial.1 = (bf16[8,64,128]{2,1,0:T(8,128)(2,1)}, bf16[8,64,128]{2,1,0:T(8,128)(2,1)}, f32[8,128]{1,0:T(8,128)}, bf16[544,128]{1,0:T(8,128)(2,1)}, bf16[2,...) custom-call(bf16[8,64,1024]{2,1,0:T(8,128)(2,1)} %get-tuple-element.127.refs_0_, ...), custom_call_target="tpu_custom_call" | custom-call | tf_op jit(solution)/shard_map/swap_partial/pallas_call | solution.py:420
  173.5 19.9 %swap_results.1 = (bf16[2,4096,128]{2,1,0:T(8,128)(2,1)}, bf16[2,256,1024]{2,1,0:T(8,128)(2,1)}, bf16[8,64,128]{2,1,0:T(8,128)(2,1)}, bf16[8,64,128]{2,1,0:T(8,1...) custom-call(bf16[8,1024,512]{2,1,0:T(8,128)(2,1)} %get-tuple-element.103.refs_5_.refs_11_, ...), custom_call_target="tpu_custom_call" | custom-call | tf_op jit(solution)/shard_map/swap_results/pallas_call | solution.py:420
  193.4 14.6 %outputs.1 = (f32[8,4096,128]{2,1,0:T(8,128)}, f32[8,256,1024]{2,1,0:T(8,128)}, bf16[512,128]{1,0:T(8,128)(2,1)}, bf16[512,128]{1,0:T(8,128)(2,1)}, f32[1,128]{1...) custom-call(bf16[2,4096,128]{2,1,0:T(8,128)(2,1)} %get-tuple-element, ...), custom_call_target="tpu_custom_call" | custom-call | tf_op jit(solution)/shard_map/outputs/pallas_call | solution.py:1220

commit v5 on v4

--- a/solution.py
+++ b/solution.py
@@ -20,7 +20,6 @@
 EVERY = ("dp", "row", "col")
 LANES = 128
 HBM = pl.BlockSpec(memory_space=pl.ANY)
-FULL = pl.BlockSpec(memory_space=pltpu.VMEM)
 TURN = LANES // 4
 
 
@@ -652,13 +651,15 @@
     mixed[...] = jnp.where(first, out[:tokens, :], out[tokens:, :]).astype(jnp.bfloat16)
 
 
-def attend_again_body(query, pair, far, start, log_total, keys, values, queries, chances):
+def attend_again_body(query, pair, far, start, log_total, queries, keys, values, queries_turned, chances):
     tokens = query.shape[0]
     last = far.shape[0]
     doubled(pair[...], keys, values, last)
     for d in range(1, last + 1):
         doubled(far[d - 1], keys, values, last - d, d)
-    queries[...] = per_head(query[...].astype(jnp.float32)).astype(jnp.bfloat16)
+    stacked = per_head(query[...].astype(jnp.float32))
+    queries[...] = stacked.astype(jnp.bfloat16)
+    queries_turned[...] = stacked.T.astype(jnp.bfloat16)
 
     def tile(rows, row, step):
         starts = start[pl.ds(pl.multiple_of(row, step), step), :]
@@ -669,11 +670,13 @@
     attend_tiles(tokens, tile)
 
 
-def attend_back_body(grad, w_output, mixed, cosine, sine, query_grad, pair_grad, far_grad, output_grad, grads, turned, key_sums, value_sums, keys, values, queries, chances):
+def attend_back_body(grad, w_output, mixed, cosine, sine, query_grad, pair_grad, far_grad, output_grad, grads, grads_turned, turned, key_sums, value_sums, keys, values, queries_turned, chances):
     tokens = mixed.shape[0]
     last = keys.shape[0] - 1
     given_grad = grad[...].reshape(tokens, -1)
-    grads[...] = per_head(dot(given_grad, w_output[...], 1, 1)).astype(jnp.bfloat16)
+    stacked = per_head(dot(given_grad, w_output[...], 1, 1))
+    grads[...] = stacked.astype(jnp.bfloat16)
+    grads_turned[...] = stacked.T.astype(jnp.bfloat16)
     output_sum = dot(mixed[...], given_grad, 0, 0).astype(jnp.bfloat16)
     for i in range(output_grad.shape[0]):
         output_grad[i] = output_sum[:, i * LANES : (i + 1) * LANES]
@@ -682,7 +685,8 @@
         cleared(value_sums.at[block])
 
     def tile(rows, row, step):
-        asked, given = queries[rows, :], grads[rows, :]
+        given = grads[rows, :]
+        asked_turned, given_turned = queries_turned[:, rows], grads_turned[:, rows]
         products = [dot(given, values[block], 1, 1) for block in range(last + 1)]
         delta = functools.reduce(
             jnp.add,
@@ -696,8 +700,8 @@
             chance = chances[block, rows, :]
             back = (chance * (products[block] - delta)).astype(jnp.bfloat16)
             total = total + dot(back, keys[block])
-            key_sums[block] += dot(back, asked, 0, 0)
-            value_sums[block] += dot(chance.astype(jnp.bfloat16), given, 0, 0)
+            key_sums[block] += dot(asked_turned, back)
+            value_sums[block] += dot(given_turned, chance.astype(jnp.bfloat16))
         turned[rows, :] = total
 
     attend_tiles(tokens, tile)
@@ -706,7 +710,7 @@
     query_grad[...] = (raw * cosine[...] - flipped(raw) * sine[...]).astype(jnp.bfloat16)
 
     def joined(block):
-        by_key, by_value = key_sums[block], value_sums[block]
+        by_key, by_value = key_sums[block].T, value_sums[block].T
         by_key = (by_key + pltpu.roll(by_key, LANES // 2, 1)) * SCORE_SCALE
         by_value = by_value + pltpu.roll(by_value, LANES // 2, 1)
         return jnp.where(first, by_key, by_value)
@@ -1131,9 +1135,14 @@
     pieces = total // count
     sums, smalls = refs[: 2 * pieces], refs[2 * pieces : 2 * pieces + 6]
     gin, gout, *others = refs[2 * pieces + 6 : 2 * pieces + 16]
-    block_out, in_grad, gain_attn, gain_moe, query, pair, output, router = others
     in_low, out_low, in_full, out_full, *refs = refs[2 * pieces + 16 :]
-    held, (load_sem, store_sem, small_sem) = refs[:6], refs[6:]
+    held, results, (load_sem, store_sem, small_sem) = refs[:6], refs[6:14], refs[14:]
+    block_out, in_grad, gain_attn, gain_moe, query, pair, output, router = results
+    width = gout.shape[2]
+    stored = [
+        pltpu.make_async_copy(a, b, small_sem.at[6 + j])
+        for j, (a, b) in enumerate(zip(results, others))
+    ]
     ring = in_full.shape[0]
 
     def load(k, i):
@@ -1159,7 +1168,6 @@
         for copy in fetched:
             copy.wait()
         blocks, in_blocks, gains, summed, output_first, output_last = held
-        width = gout.shape[2]
         for i in range(blocks.shape[0]):
             at = pl.ds(i * blocks.shape[1], blocks.shape[1])
             block_out[at, :] = blocks[i]
@@ -1192,9 +1200,13 @@
             store(k, i).start()
         if i == total - 3:
             small()
+            for copy in stored:
+                copy.start()
     for i in range(total - ring, total):
         for k in range(2):
             store(k, i).wait()
+    for copy in stored:
+        copy.wait()
 
 
 def outputs(in_sums, out_sums, hidden, experts, *smalls):
@@ -1220,12 +1232,13 @@
     gin, *others = pl.pallas_call(
         functools.partial(outputs_body, count, total),
         in_specs=[HBM] * (2 * len(in_sums) + len(smalls)),
-        out_specs=(HBM, HBM) + (FULL,) * (len(shapes) - 2),
+        out_specs=(HBM,) * len(shapes),
         out_shape=tuple(jax.ShapeDtypeStruct(*shape) for shape in shapes),
         scratch_shapes=[pltpu.VMEM((total,) + s, low) for s in large]
         + [pltpu.VMEM((ring,) + s, full) for s in large]
         + [pltpu.VMEM(a.shape, a.dtype) for a in smalls]
-        + [pltpu.SemaphoreType.DMA(s) for s in ((2, total), (2, ring), (len(smalls),))],
+        + [pltpu.VMEM(*shape) for shape in shapes[2:]]
+        + [pltpu.SemaphoreType.DMA(s) for s in ((2, total), (2, ring), (14,))],
         name="outputs",
     )(*in_sums, *out_sums, *smalls)
     gin = gin.reshape(total, width, parts, 2, LANES).transpose(0, 1, 3, 2, 4)
@@ -1420,7 +1433,16 @@
         ("gather", attn_grad, False, 2),
         ("gather", logit_grad),
         delayed=(1,),
-        before=Stage(attend_again_body, [], query, pair, far, start, log_total),
+        before=Stage(
+            attend_again_body,
+            [],
+            query,
+            pair,
+            far,
+            start,
+            log_total,
+            scratch=[pltpu.VMEM(twice, low)],
+        ),
         after=Stage(
             attend_back_body,
             [
@@ -1436,16 +1458,17 @@
             sine,
             scratch=[
                 pltpu.VMEM(twice, low),
+                pltpu.VMEM(twice[::-1], low),
                 pltpu.VMEM(twice, full),
-                pltpu.VMEM(stack, full),
-                pltpu.VMEM(stack, full),
+                pltpu.VMEM((hop_count + 1,) + turned_block, full),
+                pltpu.VMEM((hop_count + 1,) + turned_block, full),
             ],
         ),
         landing=(0,),
         shared=[
             pltpu.VMEM(stack, low),
             pltpu.VMEM(stack, low),
-            pltpu.VMEM(twice, low),
+            pltpu.VMEM(twice[::-1], low),
             pltpu.VMEM((hop_count + 1, 2 * tok_rows, tok_rows), full),
         ],
     )

time: 208 us -> 207 us (level)
  no operation moved by 1% of the time
where the time goes in v5:
time: 207 us; the launch traced here: 206 us
  Pallas kernels  206 us (100%)
    pallas_call x9, Pallas kernels, exchange(): pl.pallas_call(body, out_shape=tuple((shape(s) for s in outs + made_shape...  157 us
    pallas_call x1, Pallas kernels, local_experts(): pl.pallas_call(functools.partial(local_experts_body, sizes, kinds), grid=...  35.3 us
    pallas_call x1, Pallas kernels, outputs(): pl.pallas_call(functools.partial(outputs_body, count, total), in_specs=[H...  13.5 us

profile of v5, /device:TPU:0, one launch (start us, length us, event | category | flops | bytes accessed | tf_op | source)
XLA Modules:
  0.0 206.4 jit_solution(16711223212650542650)
XLA Ops:
  0.6 21.7 %gather_tokens.1 = (f32[512,128]{1,0:T(8,128)}, f32[512,128]{1,0:T(8,128)}, bf16[512,1024]{1,0:T(8,128)(2,1)}, bf16[512,128]{1,0:T(8,128)(2,1)}, bf16[512,128]{1...) custom-call(bf16[1024,128]{1,0:T(8,128)(2,1)} %refs_3_.1, ...), custom_call_target="tpu_custom_call" | custom-call | tf_op jit(solution)/shard_map/gather_tokens/pallas_call | solution.py:419
  22.3 16.3 %shift_pairs.1 = (bf16[64,1024]{1,0:T(8,128)(2,1)}, bf16[8,128,512]{2,1,0:T(8,128)(2,1)}, bf16[3,128,512]{2,1,0:T(8,128)(2,1)}, s32[512,1]{1,0:T(8,128)}, bf16[5...) custom-call(bf16[8,512,128]{2,1,0:T(8,128)(2,1)} %get-tuple-element.85.ref, ...), custom_call_target="tpu_custom_call" | custom-call | tf_op jit(solution)/shard_map/shift_pairs/pallas_call | solution.py:419
  38.6 7.4 %swap_mixed.1 = (bf16[64,1152]{1,0:T(8,128)(2,1)}, f32[64,1024]{1,0:T(8,128)}, f32[64,128]{1,0:T(8,128)}) custom-call(bf16[64,1024]{1,0:T(8,128)(2,1)} %get-tuple-element.91.refs_0_.refs_1_, bf16[1024,1024]{1,0:T(8,128)(2,1)} %bitcast.45, bf16[8,1,128]{2,1,0:T(2,128)(2,1)} %get-tuple-element.93.refs_2_.refs_3_, ...), custom_call_target="tpu_custom_call" | custom-call | tf_op jit(solution)/shard_map/swap_mixed/pallas_call | solution.py:419
  46.0 15.7 %gather_rows.1 = (bf16[8,64,1152]{2,1,0:T(8,128)(2,1)}, bf16[3,64,1152]{2,1,0:T(8,128)(2,1)}) custom-call(bf16[64,1152]{1,0:T(8,128)(2,1)} %get-tuple-element.98.refs_0_.refs_1_, bf16[64,1152]{1,0:T(8,128)(2,1)} %get-tuple-element.98.refs_0_.refs_1_), custom_call_target="tpu_custom_call" | custom-call | tf_op jit(solution)/shard_map/gather_rows/pallas_call | solution.py:419
  61.7 35.3 %local_experts.1 = (bf16[8,1024,512]{2,1,0:T(8,128)(2,1)}, bf16[8,512,1024]{2,1,0:T(8,128)(2,1)}, bf16[8,256,1024]{2,1,0:T(8,128)(2,1)}, bf16[512,1024]{1,0:T(8,...) custom-call(bf16[512,1152]{1,0:T(8,128)(2,1)} %bitcast.43, ...), custom_call_target="tpu_custom_call" | custom-call | tf_op jit(solution)/shard_map/local_experts/pallas_call | solution.py:948
  97.0 17.9 %swap_back.1 = (f32[64,1024]{1,0:T(8,128)}, bf16[64,1024]{1,0:T(8,128)(2,1)}, bf16[64,128]{1,0:T(8,128)(2,1)}, f32[1,1024]{1,0:T(1,128)}, bf16[2,4096,128]{2,1,0:T(8,128)(2,1)}, /*index=5*/bf16[2,256,1024]{2,1,0:T(8,128)(2,1)}) custom-call(bf16[64,1024]{1,0:T(8,128)(2,1)} %get-tuple-element.90.refs_0_, f32[64,1024]{1,0:T(8,128)} %get-tuple-element.96.refs_1_.refs_2_, ...), custom_call_target="tpu_custom_call" | custom-call | tf_op jit(solution)/shard_map/swap_back/pallas_call | solution.py:419
  114.9 18.1 %gather_attn_grad.1 = (bf16[512,128]{1,0:T(8,128)(2,1)}, f32[512,128]{1,0:T(8,128)}, bf16[2,512,128]{2,1,0:T(8,128)(2,1)}, bf16[8,128,128]{2,1,0:T(8,128)(2,1)}, bf16[8,64,128]{2,1,0:T(8,128)(2,1)}) custom-call(bf16[512,128]{1,0:T(8,128)(2,1)} %get-tuple-element.87.refs_2_.refs_0_, bf16[512,128]{1,0:T(8,128)(2,1)} %get-tuple-element.88.refs_3_.refs_6_.refs_1_, ...), custom_call_target="tpu_custom_call" | custom-call | tf_op jit(solution)/shard_map/gather_attn_grad/pallas_call | solution.py:419
  133.0 20.5 %shift_grads.1 = (bf16[512,1024]{1,0:T(8,128)(2,1)}, bf16[2176,128]{1,0:T(8,128)(2,1)}, bf16[128,128]{1,0:T(8,128)(2,1)}, bf16[128,128]{1,0:T(8,128)(2,1)}, f32[...) custom-call(bf16[512,128]{1,0:T(8,128)(2,1)} %get-tuple-element.117., ...), custom_call_target="tpu_custom_call" | custom-call | tf_op jit(solution)/shard_map/shift_grads/pallas_call | solution.py:419
  153.5 19.2 %swap_partial.1 = (bf16[8,64,128]{2,1,0:T(8,128)(2,1)}, bf16[8,64,128]{2,1,0:T(8,128)(2,1)}, f32[8,128]{1,0:T(8,128)}, bf16[544,128]{1,0:T(8,128)(2,1)}, bf16[2,...) custom-call(bf16[8,64,1024]{2,1,0:T(8,128)(2,1)} %get-tuple-element.127.refs_0_, ...), custom_call_target="tpu_custom_call" | custom-call | tf_op jit(solution)/shard_map/swap_partial/pallas_call | solution.py:419
  172.7 20.0 %swap_results.1 = (bf16[2,4096,128]{2,1,0:T(8,128)(2,1)}, bf16[2,256,1024]{2,1,0:T(8,128)(2,1)}, bf16[8,64,128]{2,1,0:T(8,128)(2,1)}, bf16[8,64,128]{2,1,0:T(8,1...) custom-call(bf16[8,1024,512]{2,1,0:T(8,128)(2,1)} %get-tuple-element.103.refs_5_.refs_11_, ...), custom_call_target="tpu_custom_call" | custom-call | tf_op jit(solution)/shard_map/swap_results/pallas_call | solution.py:419
  192.7 13.5 %outputs.1 = (f32[8,4096,128]{2,1,0:T(8,128)}, f32[8,256,1024]{2,1,0:T(8,128)}, bf16[512,128]{1,0:T(8,128)(2,1)}, bf16[512,128]{1,0:T(8,128)(2,1)}, f32[1,128]{1...) custom-call(bf16[2,4096,128]{2,1,0:T(8,128)(2,1)} %get-tuple-element, ...), custom_call_target="tpu_custom_call" | custom-call | tf_op jit(solution)/shard_map/outputs/pallas_call | solution.py:1232

commit v6 on v5

--- a/solution.py
+++ b/solution.py
@@ -820,7 +820,9 @@
     output_last[...] = output_sum[output_first.shape[0] :, :]
     mine = rows[:, own_rows(LANES)]
     named = logit[...].reshape(normed.shape[0], LANES)
-    sums[2 * width : 2 * width + LANES, :] = dot(named, mine, 0, 0).astype(jnp.bfloat16)
+    router_sum = dot(named, mine, 0, 0).astype(jnp.bfloat16)
+    count = min(LANES, sums.shape[0] - 2 * width)
+    sums[2 * width : 2 * width + count, :] = router_sum[:count, :]
 
 
 def results_body(blocks, moe, own, middle, middle_grad, gains, gain_blocks, turned, block_out, in_grad, gain_sum, summed):
@@ -1472,13 +1474,13 @@
             pltpu.VMEM((hop_count + 1, 2 * tok_rows, tok_rows), full),
         ],
     )
-    length = (2 * width + LANES + unit - 1) // unit * unit
+    length = (2 * width + experts + unit - 1) // unit * unit
     partial, sums, output_first, output_last, gain_parts, moe_blocks = beneath(
         "shift_grads",
         6,
         ("shift", far_grad, [-d for d in hops], True),
+        ("turn", output_sum.reshape(depth, width // depth, LANES)),
         ("swap", moe_partial.reshape(group, own, width)),
-        ("turn", output_sum.reshape(depth, width // depth, LANES)),
         after=Stage(
             project_back_body,
             [
@@ -1496,44 +1498,44 @@
             w_pair,
             cosine,
             sine,
-            Got(2),
+            Got(1),
             logit_blocks,
             rows_near,
             gains,
             gain_moe_part,
         ),
-        landing=(0, 2),
+        landing=(0, 1),
     )
     pieces = (group, own, LANES)
     block_out, in_grad, gain_sum, summed, output_first = beneath(
         "swap_partial",
         7,
+        ("turn", sums.reshape(depth, length // depth, LANES)),
+        ("collect", output_first),
         ("swap", partial.reshape(group, own, width)),
-        ("turn", sums.reshape(depth, length // depth, LANES)),
         ("swap", gain_parts),
-        ("collect", output_first),
         after=Stage(
             results_body,
             [(pieces, low), (pieces, low), ((8, LANES), full), ((length // depth, LANES), low)],
-            Got(0),
+            Got(2),
             moe_blocks,
             tokens_own,
             middle,
             middle_grad,
             gains,
-            Got(2),
-            Got(1),
+            Got(3),
+            Got(0),
         ),
-        landing=(0, 1, 2),
-    )
-    block_out, in_grad, sums, output_last, gain_all = beneath(
+        landing=(0, 2, 3),
+    )
+    sums, output_last, gain_all, block_out, in_grad = beneath(
         "swap_results",
         8,
-        ("swap", block_out),
-        ("swap", in_grad),
         ("collect", summed),
         ("collect", output_last),
         ("collect", gain_sum),
+        ("swap", block_out),
+        ("swap", in_grad),
     )
     grad_in, grad_out, block_out, in_grad, gain_attn_sum, gain_moe_sum, query_sum, pair_sum, output_sum, router_sum = outputs(
         in_sums,

time: 207 us -> 206 us (level)
  no operation moved by 1% of the time
where the time goes in v6:
time: 206 us
  Pallas kernels  205 us (100%)
    pallas_call x9, Pallas kernels, exchange(): pl.pallas_call(body, out_shape=tuple((shape(s) for s in outs + made_shape...  156 us
    pallas_call x1, Pallas kernels, local_experts(): pl.pallas_call(functools.partial(local_experts_body, sizes, kinds), grid=...  35.3 us
    pallas_call x1, Pallas kernels, outputs(): pl.pallas_call(functools.partial(outputs_body, count, total), in_specs=[H...  13.5 us

profile of v6, /device:TPU:0, one launch (start us, length us, event | category | flops | bytes accessed | tf_op | source)
XLA Modules:
  0.0 205.9 jit_solution(13961651063990692743)
XLA Ops:
  0.6 21.7 %gather_tokens.1 = (f32[512,128]{1,0:T(8,128)}, f32[512,128]{1,0:T(8,128)}, bf16[512,1024]{1,0:T(8,128)(2,1)}, bf16[512,128]{1,0:T(8,128)(2,1)}, bf16[512,128]{1...) custom-call(bf16[1024,128]{1,0:T(8,128)(2,1)} %refs_3_.1, ...), custom_call_target="tpu_custom_call" | custom-call | tf_op jit(solution)/shard_map/gather_tokens/pallas_call | solution.py:419
  22.3 16.3 %shift_pairs.1 = (bf16[64,1024]{1,0:T(8,128)(2,1)}, bf16[8,128,512]{2,1,0:T(8,128)(2,1)}, bf16[3,128,512]{2,1,0:T(8,128)(2,1)}, s32[512,1]{1,0:T(8,128)}, bf16[5...) custom-call(bf16[8,512,128]{2,1,0:T(8,128)(2,1)} %get-tuple-element.85.ref, ...), custom_call_target="tpu_custom_call" | custom-call | tf_op jit(solution)/shard_map/shift_pairs/pallas_call | solution.py:419
  38.6 7.4 %swap_mixed.1 = (bf16[64,1152]{1,0:T(8,128)(2,1)}, f32[64,1024]{1,0:T(8,128)}, f32[64,128]{1,0:T(8,128)}) custom-call(bf16[64,1024]{1,0:T(8,128)(2,1)} %get-tuple-element.91.refs_0_.refs_1_, bf16[1024,1024]{1,0:T(8,128)(2,1)} %bitcast.45, bf16[8,1,128]{2,1,0:T(2,128)(2,1)} %get-tuple-element.93.refs_2_.refs_3_, ...), custom_call_target="tpu_custom_call" | custom-call | tf_op jit(solution)/shard_map/swap_mixed/pallas_call | solution.py:419
  46.0 15.7 %gather_rows.1 = (bf16[8,64,1152]{2,1,0:T(8,128)(2,1)}, bf16[3,64,1152]{2,1,0:T(8,128)(2,1)}) custom-call(bf16[64,1152]{1,0:T(8,128)(2,1)} %get-tuple-element.98.refs_0_.refs_1_, bf16[64,1152]{1,0:T(8,128)(2,1)} %get-tuple-element.98.refs_0_.refs_1_), custom_call_target="tpu_custom_call" | custom-call | tf_op jit(solution)/shard_map/gather_rows/pallas_call | solution.py:419
  61.7 35.3 %local_experts.1 = (bf16[8,1024,512]{2,1,0:T(8,128)(2,1)}, bf16[8,512,1024]{2,1,0:T(8,128)(2,1)}, bf16[8,256,1024]{2,1,0:T(8,128)(2,1)}, bf16[512,1024]{1,0:T(8,...) custom-call(bf16[512,1152]{1,0:T(8,128)(2,1)} %bitcast.43, ...), custom_call_target="tpu_custom_call" | custom-call | tf_op jit(solution)/shard_map/local_experts/pallas_call | solution.py:950
  97.0 17.9 %swap_back.1 = (f32[64,1024]{1,0:T(8,128)}, bf16[64,1024]{1,0:T(8,128)(2,1)}, bf16[64,128]{1,0:T(8,128)(2,1)}, f32[1,1024]{1,0:T(1,128)}, bf16[2,4096,128]{2,1,0:T(8,128)(2,1)}, /*index=5*/bf16[2,256,1024]{2,1,0:T(8,128)(2,1)}) custom-call(bf16[64,1024]{1,0:T(8,128)(2,1)} %get-tuple-element.90.refs_0_, f32[64,1024]{1,0:T(8,128)} %get-tuple-element.96.refs_1_.refs_2_, ...), custom_call_target="tpu_custom_call" | custom-call | tf_op jit(solution)/shard_map/swap_back/pallas_call | solution.py:419
  114.9 18.1 %gather_attn_grad.1 = (bf16[512,128]{1,0:T(8,128)(2,1)}, f32[512,128]{1,0:T(8,128)}, bf16[2,512,128]{2,1,0:T(8,128)(2,1)}, bf16[8,128,128]{2,1,0:T(8,128)(2,1)}, bf16[8,64,128]{2,1,0:T(8,128)(2,1)}) custom-call(bf16[512,128]{1,0:T(8,128)(2,1)} %get-tuple-element.87.refs_2_.refs_0_, bf16[512,128]{1,0:T(8,128)(2,1)} %get-tuple-element.88.refs_3_.refs_6_.refs_1_, ...), custom_call_target="tpu_custom_call" | custom-call | tf_op jit(solution)/shard_map/gather_attn_grad/pallas_call | solution.py:419
  133.0 20.5 %shift_grads.1 = (bf16[512,1024]{1,0:T(8,128)(2,1)}, bf16[2112,128]{1,0:T(8,128)(2,1)}, bf16[128,128]{1,0:T(8,128)(2,1)}, bf16[128,128]{1,0:T(8,128)(2,1)}, f32[...) custom-call(bf16[512,128]{1,0:T(8,128)(2,1)} %get-tuple-element.117., ...), custom_call_target="tpu_custom_call" | custom-call | tf_op jit(solution)/shard_map/shift_grads/pallas_call | solution.py:419
  153.5 19.2 %swap_partial.1 = (bf16[8,64,128]{2,1,0:T(8,128)(2,1)}, bf16[8,64,128]{2,1,0:T(8,128)(2,1)}, f32[8,128]{1,0:T(8,128)}, bf16[528,128]{1,0:T(8,128)(2,1)}, bf16[2,...) custom-call(bf16[8,64,1024]{2,1,0:T(8,128)(2,1)} %get-tuple-element.127.refs_0_, ...), custom_call_target="tpu_custom_call" | custom-call | tf_op jit(solution)/shard_map/swap_partial/pallas_call | solution.py:419
  172.7 19.5 %swap_results.1 = (bf16[2,4096,128]{2,1,0:T(8,128)(2,1)}, bf16[2,256,1024]{2,1,0:T(8,128)(2,1)}, bf16[4,528,128]{2,1,0:T(8,128)(2,1)}, bf16[4,128,128]{2,1,0:T(8...) custom-call(bf16[8,1024,512]{2,1,0:T(8,128)(2,1)} %get-tuple-element.103.refs_5_.refs_11_, ...), custom_call_target="tpu_custom_call" | custom-call | tf_op jit(solution)/shard_map/swap_results/pallas_call | solution.py:419
  192.2 13.5 %outputs.1 = (f32[8,4096,128]{2,1,0:T(8,128)}, f32[8,256,1024]{2,1,0:T(8,128)}, bf16[512,128]{1,0:T(8,128)(2,1)}, bf16[512,128]{1,0:T(8,128)(2,1)}, f32[1,128]{1...) custom-call(bf16[2,4096,128]{2,1,0:T(8,128)(2,1)} %get-tuple-element, ...), custom_call_target="tpu_custom_call" | custom-call | tf_op jit(solution)/shard_map/outputs/pallas_call | solution.py:1234

commit v7 on v6

--- a/solution.py
+++ b/solution.py
@@ -884,11 +884,11 @@
         share[...] = jnp.zeros_like(share)
         weights[...] = weight_rows(rows_ref[:, width:])
 
-    @pl.when(step == 2 * steps // 8)
+    @pl.when(step == steps // 8)
     def _():
         moves.start([1])
 
-    for when, item, stage in ((3, 0, 0), (6, 1, 0), (7, 0, 1)):
+    for when, item, stage in ((3, 0, 0), (5, 1, 0), (7, 0, 1)):
 
         @pl.when(step == when * steps // 8)
         def _(item=item, stage=stage):

time: 206 us -> 208 us (level)
  no operation moved by 1% of the time
where the time goes in v7:
time: 208 us
  Pallas kernels  207 us (100%)
    pallas_call x9, Pallas kernels, exchange(): pl.pallas_call(body, out_shape=tuple((shape(s) for s in outs + made_shape...  157 us
    pallas_call x1, Pallas kernels, local_experts(): pl.pallas_call(functools.partial(local_experts_body, sizes, kinds), grid=...  36.9 us
    pallas_call x1, Pallas kernels, outputs(): pl.pallas_call(functools.partial(outputs_body, count, total), in_specs=[H...  13.5 us

profile of v7, /device:TPU:0, one launch (start us, length us, event | category | flops | bytes accessed | tf_op | source)
XLA Modules:
  0.0 208.2 jit_solution(14300087313392171184)
XLA Ops:
  0.6 21.7 %gather_tokens.1 = (f32[512,128]{1,0:T(8,128)}, f32[512,128]{1,0:T(8,128)}, bf16[512,1024]{1,0:T(8,128)(2,1)}, bf16[512,128]{1,0:T(8,128)(2,1)}, bf16[512,128]{1...) custom-call(bf16[1024,128]{1,0:T(8,128)(2,1)} %refs_3_.1, ...), custom_call_target="tpu_custom_call" | custom-call | tf_op jit(solution)/shard_map/gather_tokens/pallas_call | solution.py:419
  22.3 16.3 %shift_pairs.1 = (bf16[64,1024]{1,0:T(8,128)(2,1)}, bf16[8,128,512]{2,1,0:T(8,128)(2,1)}, bf16[3,128,512]{2,1,0:T(8,128)(2,1)}, s32[512,1]{1,0:T(8,128)}, bf16[5...) custom-call(bf16[8,512,128]{2,1,0:T(8,128)(2,1)} %get-tuple-element.85.ref, ...), custom_call_target="tpu_custom_call" | custom-call | tf_op jit(solution)/shard_map/shift_pairs/pallas_call | solution.py:419
  38.6 7.4 %swap_mixed.1 = (bf16[64,1152]{1,0:T(8,128)(2,1)}, f32[64,1024]{1,0:T(8,128)}, f32[64,128]{1,0:T(8,128)}) custom-call(bf16[64,1024]{1,0:T(8,128)(2,1)} %get-tuple-element.91.refs_0_.refs_1_, bf16[1024,1024]{1,0:T(8,128)(2,1)} %bitcast.45, bf16[8,1,128]{2,1,0:T(2,128)(2,1)} %get-tuple-element.93.refs_2_.refs_3_, ...), custom_call_target="tpu_custom_call" | custom-call | tf_op jit(solution)/shard_map/swap_mixed/pallas_call | solution.py:419
  46.0 15.7 %gather_rows.1 = (bf16[8,64,1152]{2,1,0:T(8,128)(2,1)}, bf16[3,64,1152]{2,1,0:T(8,128)(2,1)}) custom-call(bf16[64,1152]{1,0:T(8,128)(2,1)} %get-tuple-element.98.refs_0_.refs_1_, bf16[64,1152]{1,0:T(8,128)(2,1)} %get-tuple-element.98.refs_0_.refs_1_), custom_call_target="tpu_custom_call" | custom-call | tf_op jit(solution)/shard_map/gather_rows/pallas_call | solution.py:419
  61.7 36.9 %local_experts.1 = (bf16[8,1024,512]{2,1,0:T(8,128)(2,1)}, bf16[8,512,1024]{2,1,0:T(8,128)(2,1)}, bf16[8,256,1024]{2,1,0:T(8,128)(2,1)}, bf16[512,1024]{1,0:T(8,...) custom-call(bf16[512,1152]{1,0:T(8,128)(2,1)} %bitcast.43, ...), custom_call_target="tpu_custom_call" | custom-call | tf_op jit(solution)/shard_map/local_experts/pallas_call | solution.py:950
  98.5 17.9 %swap_back.1 = (f32[64,1024]{1,0:T(8,128)}, bf16[64,1024]{1,0:T(8,128)(2,1)}, bf16[64,128]{1,0:T(8,128)(2,1)}, f32[1,1024]{1,0:T(1,128)}, bf16[2,4096,128]{2,1,0:T(8,128)(2,1)}, /*index=5*/bf16[2,256,1024]{2,1,0:T(8,128)(2,1)}) custom-call(bf16[64,1024]{1,0:T(8,128)(2,1)} %get-tuple-element.90.refs_0_, f32[64,1024]{1,0:T(8,128)} %get-tuple-element.96.refs_1_.refs_2_, ...), custom_call_target="tpu_custom_call" | custom-call | tf_op jit(solution)/shard_map/swap_back/pallas_call | solution.py:419
  116.4 19.0 %gather_attn_grad.1 = (bf16[512,128]{1,0:T(8,128)(2,1)}, f32[512,128]{1,0:T(8,128)}, bf16[2,512,128]{2,1,0:T(8,128)(2,1)}, bf16[8,128,128]{2,1,0:T(8,128)(2,1)}, bf16[8,64,128]{2,1,0:T(8,128)(2,1)}) custom-call(bf16[512,128]{1,0:T(8,128)(2,1)} %get-tuple-element.87.refs_2_.refs_0_, bf16[512,128]{1,0:T(8,128)(2,1)} %get-tuple-element.88.refs_3_.refs_6_.refs_1_, ...), custom_call_target="tpu_custom_call" | custom-call | tf_op jit(solution)/shard_map/gather_attn_grad/pallas_call | solution.py:419
  135.5 20.5 %shift_grads.1 = (bf16[512,1024]{1,0:T(8,128)(2,1)}, bf16[2112,128]{1,0:T(8,128)(2,1)}, bf16[128,128]{1,0:T(8,128)(2,1)}, bf16[128,128]{1,0:T(8,128)(2,1)}, f32[...) custom-call(bf16[512,128]{1,0:T(8,128)(2,1)} %get-tuple-element.117., ...), custom_call_target="tpu_custom_call" | custom-call | tf_op jit(solution)/shard_map/shift_grads/pallas_call | solution.py:419
  155.9 19.2 %swap_partial.1 = (bf16[8,64,128]{2,1,0:T(8,128)(2,1)}, bf16[8,64,128]{2,1,0:T(8,128)(2,1)}, f32[8,128]{1,0:T(8,128)}, bf16[528,128]{1,0:T(8,128)(2,1)}, bf16[2,...) custom-call(bf16[8,64,1024]{2,1,0:T(8,128)(2,1)} %get-tuple-element.127.refs_0_, ...), custom_call_target="tpu_custom_call" | custom-call | tf_op jit(solution)/shard_map/swap_partial/pallas_call | solution.py:419
  175.1 19.4 %swap_results.1 = (bf16[2,4096,128]{2,1,0:T(8,128)(2,1)}, bf16[2,256,1024]{2,1,0:T(8,128)(2,1)}, bf16[4,528,128]{2,1,0:T(8,128)(2,1)}, bf16[4,128,128]{2,1,0:T(8...) custom-call(bf16[8,1024,512]{2,1,0:T(8,128)(2,1)} %get-tuple-element.103.refs_5_.refs_11_, ...), custom_call_target="tpu_custom_call" | custom-call | tf_op jit(solution)/shard_map/swap_results/pallas_call | solution.py:419
  194.5 13.5 %outputs.1 = (f32[8,4096,128]{2,1,0:T(8,128)}, f32[8,256,1024]{2,1,0:T(8,128)}, bf16[512,128]{1,0:T(8,128)(2,1)}, bf16[512,128]{1,0:T(8,128)(2,1)}, f32[1,128]{1...) custom-call(bf16[2,4096,128]{2,1,0:T(8,128)(2,1)} %get-tuple-element, ...), custom_call_target="tpu_custom_call" | custom-call | tf_op jit(solution)/shard_map/outputs/pallas_call | solution.py:1234
